TPU v7x, 16 devices: a whole 2x2x2 slice. The times are simulated.
16 devices in a mesh: rep: 2 (over z), nodes: 8 (over y, x, core).
Axes of the slice: x: 2, y: 2, z: 2, core: 2. Of those that a mesh axis runs over, the one named last changes fastest.
Arguments:
- adjacency: bfloat16 [16384, 16384], P('nodes')
- features: bfloat16 [16384, 100], P(('nodes', 'rep'))
- w_one: float32 [100, 256], replicated
- w_two: float32 [256, 47], replicated
- labels: int32 [16384], P(('nodes', 'rep'))
- label_mask: int32 [16384], P(('nodes', 'rep'))
Outputs:
- output 1: float32 [], replicated
- output 2: float32 [100, 256], replicated
- output 3: float32 [256, 47], replicated
All inputs are finite; a program needn't handle non-finite values.
Results may differ from a plain program's by a relative error of at most 0.001.
Values are sent between devices in bfloat16 or wider.
A program may use at most 1 GiB of HBM per device.

v0:
```python
import jax
import jax.numpy as jnp
from jax import lax
from jax.sharding import PartitionSpec as P


def solution(mesh):
    rep_size = mesh.shape["rep"]
    node_size = mesh.shape["nodes"]
    all_axes = ("rep", "nodes")

    def local_step(adj_rows, features, w_one, w_two, labels, label_mask):
        rows_dev = features.shape[0]
        group_rows_n = adj_rows.shape[0]
        num_classes = w_two.shape[1]
        adj_split = adj_rows.reshape(group_rows_n, node_size, rep_size, rows_dev)
        adj_mine = lax.dynamic_index_in_dim(adj_split, lax.axis_index("rep"), axis=2, keepdims=False)

        def aggregate(values):
            gathered = lax.all_gather(values, "nodes")
            partial_sum = jnp.einsum("ajb,jbf->af", adj_mine, gathered, preferred_element_type=jnp.float32)
            return lax.psum_scatter(partial_sum, "rep", scatter_dimension=0, tiled=True)

        def aggregate_t(grad_rows):
            group_grads = lax.all_gather(grad_rows, "rep", tiled=True)
            partial_sum = jnp.einsum("ajb,af->jbf", adj_mine, group_grads, preferred_element_type=jnp.float32)
            return lax.psum_scatter(partial_sum, "nodes", scatter_dimension=0, tiled=False)

        w_one_b = w_one.astype(jnp.bfloat16)
        w_two_b = w_two.astype(jnp.bfloat16)
        y_one = jnp.dot(features, w_one_b, preferred_element_type=jnp.float32).astype(jnp.bfloat16)
        z_one = aggregate(y_one)
        h_one = jnp.maximum(z_one, 0.0).astype(jnp.bfloat16)
        y_two = jnp.dot(h_one, w_two_b, preferred_element_type=jnp.float32).astype(jnp.bfloat16)
        z_two = aggregate(y_two)
        log_probs = jax.nn.log_softmax(z_two, axis=-1)
        onehot = (labels[:, None] == jnp.arange(num_classes)[None, :]).astype(jnp.float32)
        mask_f = label_mask.astype(jnp.float32)
        local_sums = jnp.stack([-jnp.sum(mask_f * jnp.sum(onehot * log_probs, axis=-1)), jnp.sum(mask_f)])
        global_sums = lax.psum(local_sums, all_axes)
        loss_value = global_sums[0] / global_sums[1]
        g_two = ((jnp.exp(log_probs) - onehot) * (mask_f / global_sums[1])[:, None]).astype(jnp.bfloat16)
        dy_two = aggregate_t(g_two).astype(jnp.bfloat16)
        dw_two = lax.psum(jnp.einsum("vh,vc->hc", h_one, dy_two, preferred_element_type=jnp.float32), all_axes)
        dh_one = jnp.einsum("vc,hc->vh", dy_two, w_two_b, preferred_element_type=jnp.float32)
        g_one = jnp.where(z_one > 0, dh_one, 0.0).astype(jnp.bfloat16)
        dy_one = aggregate_t(g_one).astype(jnp.bfloat16)
        dw_one = lax.psum(jnp.einsum("vf,vh->fh", features, dy_one, preferred_element_type=jnp.float32), all_axes)
        return loss_value, dw_one, dw_two

    row_spec = P(("nodes", "rep"))
    return jax.shard_map(local_step, mesh=mesh, in_specs=(P("nodes", None), P(("nodes", "rep"), None), P(), P(), row_spec, row_spec), out_specs=(P(), P(), P()), check_vma=False)
```

profile of v0, /device:TPU:0, one launch (start us, length us, event | category | flops | bytes accessed | tf_op | source)
XLA Modules:
  0.0 601.3 jit_solution(4148622914579929449)
XLA Ops:
  8.1 2.0 convolution_convert_fusion
  10.2 107.2 %reshape.18 = bf16[2048,8,2,1024]{3,2,1,0:T(2,128)(2,1)} reshape(bf16[2048,16384]{1,0:T(8,128)(2,1)} %param.6) | data formatting | bytes 134217728 | tf_op jit(solution)/shard_map/reshape | solution.py:16
  117.4 82.4 %constant_dynamic-slice_fusion = bf16[2048,8,1,1024]{3,2,1,0:T(2,128)(2,1)} fusion(bf16[2048,8,2,1024]{3,2,1,0:T(2,128)(2,1)} %reshape.18, s32[]{:T(128)S(6)} %select_n.8), kind=kLoop, calls=%fused_computation.33 | loop fusion | bytes 67108864 | tf_op jit(solution)/shard_map/jit(dynamic_index_in_dim)/dynamic_slice | solution.py:17
  199.8 34.0 %copy.18 = bf16[2048,8,1,1024]{3,0,1,2:T(8,128)(2,1)} copy(bf16[2048,8,1,1024]{3,2,1,0:T(2,128)(2,1)} %constant_dynamic-slice_fusion) | data formatting | bytes 67108864
  233.8 17.3 %convolution_bitcast_fusion = f32[2048,256]{1,0:T(8,128)} fusion(bf16[2048,8,1024]{2,0,1:T(8,128)(2,1)} %bitcast.41, bf16[8,1024,256]{2,1,0:T(8,128)(2,1)} %bitcast.47), kind=kOutput, calls=%fused_computation.1 | convolution fusion | flops 8589934592 | bytes 39845888 | tf_op jit(solution)/shard_map/ajb,jbf->af/dot_general | solution.py:21
  251.2 32.9 %reduce-scatter.5.cloned.1.call-done = f32[1024,256]{1,0:T(8,128)} async-done(((f32[2048,256]{1,0:T(8,128)}), f32[1024,256]{1,0:T(8,128)}) %reduce-scatter.5.cloned.1.call-update) | async-done | bytes 1048592 | tf_op jit(solution)/shard_map/reduce_scatter | solution.py:22
  284.1 1.5 convolution_convert_fusion.1
  285.6 10.4 %all-gather.1 = bf16[8192,47]{0,1:T(8,128)(2,1)S(1)} all-gather(bf16[1024,47]{0,1:T(8,128)(2,1)S(1)} %convolution_convert_fusion.1), channel_id=3, replica_groups=mesh['rep'=2,'nodes'=8] {'nodes'}, dimensions={0}, use_global_device_ids=true | all-gather | bytes 866304 | tf_op jit(solution)/shard_map/all_gather | solution.py:20
  296.5 16.7 %convolution_bitcast_fusion.1 = f32[2048,47]{0,1:T(8,128)} fusion(bf16[2048,8,1024]{2,0,1:T(8,128)(2,1)} %bitcast.42, bf16[8,1024,47]{1,0,2:T(8,128)(2,1)S(1)} %slice_bitcast_fusion), kind=kOutput, calls=%fused_computation.2 | convolution fusion | flops 1577058304 | bytes 34709504 | tf_op jit(solution)/shard_map/ajb,jbf->af/dot_general | solution.py:21
  313.3 10.4 %reduce-scatter.7.cloned.1.call-done = f32[1024,47]{0,1:T(8,128)} async-done(((f32[2048,47]{0,1:T(8,128)}), f32[1024,47]{0,1:T(8,128)}) %reduce-scatter.7.cloned.1.call-update) | async-done | bytes 192528 | tf_op jit(solution)/shard_map/reduce_scatter | solution.py:22
  325.6 1.0 select_reduce_fusion
  328.6 32.0 %psum.21 = f32[2]{0:T(128)S(1)} all-reduce(f32[2]{0:T(128)S(1)} %pad_maximum_fusion), channel_id=1, replica_groups=mesh['rep'=2,'nodes'=8] {'rep','nodes'}, use_global_device_ids=true, to_apply=%region_7.8 | all-reduce | flops 2 | bytes 16 | tf_op jit(solution)/shard_map/psum | solution.py:40
  361.8 1.0 multiply_convert_fusion
  362.8 5.5 all_gather.22
  368.3 16.3 %fusion.7 = f32[8,1024,47]{1,2,0:T(8,128)} fusion(bf16[2048,8,1024]{2,0,1:T(8,128)(2,1)} %bitcast.43, bf16[2048,47]{0,1:T(8,128)(2,1)S(1)} %all_gather.22), kind=kOutput, calls=%fused_computation.16 | convolution fusion | flops 1577058304 | bytes 35287040 | tf_op jit(solution)/shard_map/ajb,af->jbf/dot_general | solution.py:26
  384.7 33.2 %reduce-scatter.9.cloned.1.call-done = f32[1,1024,47]{1,2,0:T(8,128)} async-done(((f32[8,1024,47]{1,2,0:T(8,128)}), f32[1,1024,47]{1,2,0:T(8,128)}) %reduce-scatter.9.cloned.1.call-update) | async-done | bytes 192528 | tf_op jit(solution)/shard_map/reduce_scatter | solution.py:27
  418.0 2.0 fusion
  420.1 19.3 %all-gather.5.cloned.1.call-done = bf16[2048,256]{1,0:T(8,128)(2,1)} async-done(((bf16[1024,256]{1,0:T(8,128)(2,1)}), bf16[2048,256]{1,0:T(8,128)(2,1)}) %all-gather.5.cloned.1.call-update) | async-done | bytes 1048592 | tf_op jit(solution)/shard_map/all_gather | solution.py:25
  439.4 17.4 %fusion.1 = f32[8,1024,256]{2,1,0:T(8,128)} fusion(bf16[2048,8,1024]{2,0,1:T(8,128)(2,1)} %bitcast.44, bf16[2048,256]{1,0:T(8,128)(2,1)} %all-gather.5.cloned.1.call-done), kind=kOutput, calls=%fused_computation.8 | convolution fusion | flops 8589934592 | bytes 42991616 | tf_op jit(solution)/shard_map/ajb,af->jbf/dot_general | solution.py:26
  458.2 63.7 %reduce-scatter.11.cloned.1.call-done = f32[1,1024,256]{2,1,0:T(8,128)} async-done(((f32[8,1024,256]{2,1,0:T(8,128)}), f32[1,1024,256]{2,1,0:T(8,128)}) %reduce-scatter.11.cloned.1.call-update) | async-done | bytes 1048592 | tf_op jit(solution)/shard_map/reduce_scatter | solution.py:27
  521.9 2.1 convolution_bitcast_fusion.2
  524.2 32.8 %psum.23 = f32[256,47]{0,1:T(8,128)} all-reduce(f32[256,47]{0,1:T(8,128)S(1)} %fusion.6), channel_id=1, replica_groups=mesh['rep'=2,'nodes'=8] {'rep','nodes'}, use_global_device_ids=true, to_apply=%region_11.12 | all-reduce | flops 12032 | bytes 96256 | tf_op jit(solution)/shard_map/psum | solution.py:44
  557.1 34.7 %all-reduce.2.cloned.1.call-done = f32[100,256]{1,0:T(8,128)} async-done(((f32[100,256]{1,0:T(8,128)}), f32[100,256]{1,0:T(8,128)}) %all-reduce.2.cloned.1.call-update) | async-done | bytes 102416 | tf_op jit(solution)/shard_map/psum | solution.py:48
  591.8 1.5 copy.20
  (37 shorter events, 6.5 us)
Async XLA Ops:
  7.2 0.9 copy-start
  7.2 226.7 %all-gather.7.cloned.1.call-start = ((), (), s32[]{:S(2)}) async-start(), calls=%async_computation.10 | async-start | bytes 4718592 | tf_op jit(solution)/shard_map/all_gather | solution.py:20
  10.2 273.9 %reduce-scatter.5.cloned.1.call-start = ((), (), s32[]{:S(2)}) async-start(), calls=%async_computation.4 | async-start | bytes 3145728 | tf_op jit(solution)/shard_map/reduce_scatter | solution.py:22
  233.8 50.2 %copy-start.3 = (f32[256,47]{0,1:T(8,128)S(1)}, f32[256,47]{0,1:T(8,128)}, u32[]{:S(2)}) copy-start(f32[256,47]{0,1:T(8,128)} %param.9) | copy-start | bytes 144388
  251.1 74.5 %copy-start.4 = (s32[1024]{0:T(1024)S(1)}, s32[1024]{0:T(1024)}, u32[]{:S(2)}) copy-start(s32[1024]{0:T(1024)} %param.10) | copy-start | bytes 12292
  251.1 75.5 %copy-start.5 = (s32[1024]{0:T(1024)S(1)}, s32[1024]{0:T(1024)}, u32[]{:S(2)}) copy-start(s32[1024]{0:T(1024)} %param.11) | copy-start | bytes 12292
  251.2 72.5 %reduce-scatter.7.cloned.1.call-start = ((), (), s32[]{:S(2)}) async-start(), calls=%async_computation.5 | async-start | bytes 589824 | tf_op jit(solution)/shard_map/reduce_scatter | solution.py:22
  296.4 121.5 %copy-start.1 = (f32[1024,256]{1,0:T(8,128)S(1)}, f32[1024,256]{1,0:T(8,128)}, u32[]{:S(2)}) copy-start(f32[1024,256]{1,0:T(8,128)} %reduce-scatter.5.cloned.1.call-done) | copy-start | bytes 3145732
  313.2 104.8 %reduce-scatter.9.cloned.1.call-start = ((), (), s32[]{:S(2)}) async-start(), calls=%async_computation.6 | async-start | bytes 1769472 | tf_op jit(solution)/shard_map/reduce_scatter | solution.py:27
  384.7 54.7 %all-gather.5.cloned.1.call-start = ((), (), s32[]{:S(2)}) async-start(), calls=%async_computation.7 | async-start | bytes 1572864 | tf_op jit(solution)/shard_map/all_gather | solution.py:25
  420.0 104.0 %copy-start.2 = (f32[1,1024,47]{1,2,0:T(8,128)S(1)}, f32[1,1024,47]{1,2,0:T(8,128)}, u32[]{:S(2)}) copy-start(f32[1,1024,47]{1,2,0:T(8,128)} %reduce-scatter.9.cloned.1.call-done) | copy-start | bytes 577540
  420.1 101.8 %reduce-scatter.11.cloned.1.call-start = ((), (), s32[]{:S(2)}) async-start(), calls=%async_computation.8 | async-start | bytes 9437184 | tf_op jit(solution)/shard_map/reduce_scatter | solution.py:27
  456.8 135.0 %all-reduce.2.cloned.1.call-start = ((), (), s32[]{:S(2)}) async-start(), calls=%async_computation.9 | async-start | bytes 212992 | tf_op jit(solution)/shard_map/psum | solution.py:48
Sparse Core Ops, SparseCore 0:
  10.3 35.3 all-gather.6
  251.3 32.7 reduce-scatter.4
  313.3 10.3 reduce-scatter.6
  384.8 33.1 reduce-scatter.8
  420.2 19.1 all-gather.4
  456.9 64.9 reduce-scatter.10
  526.7 65.0 all-reduce.1
where the time goes:
time: 605 us; the launch traced here: 601 us
  local copies, waits for them, and re-layouts  227 us (38%)
  waiting for transfers between devices  194 us (32%)
  blocking collectives  80.7 us (13%)
  matrix products  75.6 us (12%)
  between operations  17.4 us (3%)
    reshape x1, local copies, waits for them, and re-layouts, local_step(): adj_split = adj_rows.reshape(group_rows_n, node_size, rep_size, rows_dev)  107 us
    reduce_scatter x2, waiting for transfers between devices, aggregate_t(): lax.psum_scatter(partial_sum, 'nodes', scatter_dimension=0, tiled=False)  96.9 us
    dynamic_slice x1, local copies, waits for them, and re-layouts, local_step(): lax.dynamic_index_in_dim(adj_split, lax.axis_index('rep'), axis=2, keepdi...  82.4 us
    reduce_scatter x2, waiting for transfers between devices, aggregate(): return lax.psum_scatter(partial_sum, 'rep', scatter_dimension=0, tiled=True)  43.3 us
    unnamed x15, local copies, waits for them, and re-layouts  36.9 us
    psum x1, waiting for transfers between devices, local_step(): lax.psum(jnp.einsum('vf,vh->fh', features, dy_one, preferred_element_type...  34.7 us
    dot_general x2, matrix products, aggregate(): jnp.einsum('ajb,jbf->af', adj_mine, gathered, preferred_element_type=jnp....  34 us
    dot_general x2, matrix products, aggregate_t(): jnp.einsum('ajb,af->jbf', adj_mine, group_grads, preferred_element_type=j...  33.7 us
  transfers between devices with their start and end apart: 7, of which 6 were waited for; matrix products, arithmetic and copies ran while one was open for 37% of the time, Pallas kernels for 0%

commit v1 on v0

v1 whole, which is shorter than its diff:
```python
import functools

import jax
import jax.numpy as jnp
from jax import lax
from jax.experimental import pallas as pl
from jax.experimental.pallas import tpu as pltpu
from jax.sharding import PartitionSpec as P

BF16 = jnp.bfloat16
F32 = jnp.float32

POS = {0: 0, 1: 1, 2: 2, 4: 3, 3: 4, 5: 5, 6: 6, 7: 7}
ORDERS = ((1, 2, 4), (2, 4, 1), (4, 1, 2))


def dot(a, b, dims=((1,), (0,))):
    return lax.dot_general(a, b, (dims, ((), ())), preferred_element_type=F32)


def step_kernel(nb, classes, f_in, cpad,
                a_hbm, x_hbm, w1_ref, w2_ref, w2t_ref, lab_ref, msk_ref,
                o1_ref, o2_ref,
                abuf, xg, y1, cnt, z1, h1t, y2g, z2, g2,
                p2out, p2sib, p2sum, p2rcv, d2, g1,
                p6out, p6sib, p6sum, r6f, r6x, r6y, d1,
                part1, part2, rb1, rb2, res1, res2,
                asem, xsem, ssem, rsem):
    r = lax.axis_index("rep")
    n = lax.axis_index("nodes")
    core = n % 2
    xc = (n // 2) % 2
    yc = n // 4
    hid = z1.shape[1]

    def flip(v, f):
        return 1 - v if f else v

    def coords(k, dc):
        rr = flip(r, k // 4)
        nn = flip(yc, (k // 2) % 2) * 4 + flip(xc, k % 2) * 2 + flip(core, dc)
        return rr, nn

    def block_id(k, dc):
        rr, nn = coords(k, dc)
        return nn * 2 + rr

    sent = []

    def send(src, dst, k, dc):
        i = len(sent)
        cp = pltpu.make_async_remote_copy(
            src_ref=src, dst_ref=dst, send_sem=ssem.at[i], recv_sem=rsem.at[i],
            device_id=coords(k, dc), device_id_type=pl.DeviceIdType.MESH)
        cp.start()
        sent.append(cp)
        return cp

    peers = [(k, dc) for k in range(8) for dc in range(2) if (k, dc) != (0, 0)]

    xload = pltpu.make_async_copy(x_hbm, xg.at[0], xsem)
    xload.start()
    loads = {}
    for k in POS:
        for dc in range(2):
            slot = POS[k] * 2 + dc
            col = pl.multiple_of(block_id(k, dc) * nb, nb)
            row = pl.multiple_of(r * nb, nb)
            cp = pltpu.make_async_copy(a_hbm.at[pl.ds(row, nb), pl.ds(col, nb)], abuf.at[slot], asem.at[slot])
            cp.start()
            loads[slot] = cp
    barrier = pltpu.get_barrier_semaphore()
    for k, dc in peers:
        pl.semaphore_signal(barrier, inc=1, device_id=coords(k, dc), device_id_type=pl.DeviceIdType.MESH)
    cnt[...] = jnp.zeros_like(cnt)
    z1[...] = jnp.zeros_like(z1)
    z2[...] = jnp.zeros_like(z2)
    pl.semaphore_wait(barrier, len(peers))
    xload.wait()

    def gather(buf, cuts, consume):
        def at(k, dc):
            return buf.at[POS[k] * 2 + dc]

        def piece(k, p):
            return buf.at[POS[k] * 2, pl.ds(cuts[p], cuts[p + 1] - cuts[p])]

        near = {k: send(at(0, 0), at(k, 0), k, 0) for k in (1, 2, 4)}
        sib = {0: send(at(0, 0), at(0, 1), 0, 1)}
        sib[0].wait_recv()
        consume(0, 2)
        two = {}
        for k in (1, 2, 4):
            near[k].wait_recv()
            for p, (d0, d1_, d2_) in enumerate(ORDERS):
                if k == d0:
                    two[(d0 + d1_, p)] = send(piece(d0, p), piece(d0 + d1_, p), d1_, 0)
                    two[(d0 + d2_, p)] = send(piece(d0, p), piece(d0 + d2_, p), d2_, 0)
                if k == d1_:
                    two[(d1_ + d2_, p)] = send(piece(d1_, p), piece(d1_ + d2_, p), d2_, 0)
            sib[k] = send(at(k, 0), at(k, 1), 0, 1)
        for k in (1, 2, 4):
            sib[k].wait_recv()
        consume(2, 8)
        three = []
        for k in (3, 6, 5):
            for p, (d0, d1_, d2_) in enumerate(ORDERS):
                two[(k, p)].wait_recv()
                if k == d0 + d1_:
                    three.append(send(piece(k, p), piece(7, p), d2_, 0))
            sib[k] = send(at(k, 0), at(k, 1), 0, 1)
        for k in (3, 6, 5):
            sib[k].wait_recv()
        consume(8, 14)
        for cp in three:
            cp.wait_recv()
        sib[7] = send(at(7, 0), at(7, 1), 0, 1)
        sib[7].wait_recv()
        consume(14, 16)

    ones = jnp.ones((16, nb), BF16)
    mrows = 256

    def z1_blocks(lo, hi):
        for s in range(lo, hi):
            loads[s].wait()

        @pl.loop(lo, hi)
        def _(s):
            xb = xg[s]
            cnt[...] += dot(ones, xb)
            y1[...] = dot(xb, w1_ref[...]).astype(BF16)
            yv = y1[...]
            for m in range(0, nb, mrows):
                z1[m:m + mrows, :] += dot(abuf[s, m:m + mrows, :], yv)

    third = (nb // 48) * 16
    gather(xg, (0, nb - 2 * third, nb - third, nb), z1_blocks)

    for m in range(0, nb, mrows):
        h1t[0, :, m:m + mrows] = jnp.maximum(z1[m:m + mrows, :], 0.0).T.astype(BF16)
    y2g[0] = dot(w2t_ref[...], h1t[0]).astype(BF16)

    reload = {}

    def z2_blocks(lo, hi):
        @pl.loop(lo, hi)
        def _(s):
            for m in range(0, nb, mrows):
                z2[m:m + mrows, 0:cpad] += dot(abuf[s, m:m + mrows, :], y2g[s], ((1,), (1,)))

        for k in range(4, 8):
            for dc in range(2):
                slot = POS[k] * 2 + dc
                if lo <= slot < hi:
                    col = pl.multiple_of(block_id(k - 4, dc) * nb, nb)
                    row = pl.multiple_of((1 - r) * nb, nb)
                    cp = pltpu.make_async_copy(a_hbm.at[pl.ds(row, nb), pl.ds(col, nb)], abuf.at[slot], asem.at[slot])
                    cp.start()
                    reload[slot] = cp

    third = cpad // 3
    gather(y2g, (0, third, 2 * third, cpad), z2_blocks)
    h1t_cp = send(h1t.at[0], h1t.at[1], 4, 0)

    z2t = z2[...].T[0:cpad, :]
    cls = lax.broadcasted_iota(jnp.int32, (cpad, nb), 0)
    zm = jnp.where(cls < classes, z2t, -jnp.inf)
    zs = zm - jnp.max(zm, axis=0, keepdims=True)
    logp = zs - jnp.log(jnp.sum(jnp.exp(zs), axis=0, keepdims=True))
    hot = cls == lab_ref[...]
    mask_f = msk_ref[...].astype(F32)
    total_m = cnt[0:1, f_in:f_in + 1]
    loss_v = -mask_f * jnp.sum(jnp.where(hot, logp, 0.0), axis=0, keepdims=True)
    loss_part = jnp.sum(loss_v, axis=1, keepdims=True) / total_m
    g2[0] = ((jnp.exp(logp) - hot.astype(F32)) * (mask_f / total_m)).astype(BF16)
    g2_cp = send(g2.at[0], g2.at[1], 4, 0)
    g2_cp.wait_recv()
    for s in reload:
        reload[s].wait()

    order = (3, 1, 2, 0)
    sib2, rcv2 = {}, {}

    def fin2(q):
        sib2[q].wait_recv()
        p2sum[q] += p2sib[q]
        if q:
            rcv2[q] = send(p2sum.at[q], p2rcv.at[q - 1], q, 0)

    def part2_of(q, dc):
        s, sp = POS[q] * 2 + dc, POS[q + 4] * 2 + dc
        return dot(g2[0], abuf[s]) + dot(g2[1], abuf[sp])

    for i, q in enumerate(order):
        p2out[q] = part2_of(q, 1)
        sib2[q] = send(p2out.at[q], p2sib.at[q], 0, 1)
        p2sum[q] = part2_of(q, 0)
        if i:
            fin2(order[i - 1])
    fin2(0)
    for q in (1, 2, 3):
        rcv2[q].wait_recv()
    d2[0] = (p2sum[0] + p2rcv[0] + p2rcv[1] + p2rcv[2]).astype(BF16)
    d2_cp = send(d2.at[0], d2.at[1], 4, 0)

    rows = hid // 16

    def reduce_start(part, rb):
        return [send(part.at[pl.ds(pl.multiple_of(block_id(k, dc) * rows, rows), rows)], rb.at[i], k, dc)
                for i, (k, dc) in enumerate(peers)]

    def reduce_mid(part, rb, res, cps):
        own = pl.ds(pl.multiple_of(block_id(0, 0) * rows, rows), rows)
        acc = part[own, :]
        for i, cp in enumerate(cps):
            cp.wait_recv()
            acc = acc + rb[i]
        res[own, :] = acc
        return [send(res.at[own], res.at[own], k, dc) for k, dc in peers]

    def g1_of(i):
        g1[i] = jnp.where(h1t[i] > 0, dot(w2_ref[...], d2[i]), 0.0).astype(BF16)

    g1_of(0)
    lane = lax.broadcasted_iota(jnp.int32, (hid, cpad), 1)
    dw2 = dot(h1t[0], d2[0], ((1,), (1,)))
    part2[...] = jnp.zeros_like(part2)
    part2[:, 0:cpad] = jnp.where(lane == classes, loss_part, dw2)
    h1t_cp.wait_recv()
    d2_cp.wait_recv()
    g1_of(1)

    half = nb // 2
    units = ((3, 0), (3, 1), (1, 0), (2, 1), (2, 0), (1, 1), (0, 0), (0, 1))
    sib6, got = {}, {}

    def part6_of(q, h, dc):
        s, sp = POS[q] * 2 + dc, POS[q + 4] * 2 + dc
        lo = h * half
        return dot(g1[0], abuf[s, :, lo:lo + half]) + dot(g1[1], abuf[sp, :, lo:lo + half])

    def fin6(i):
        q, h = units[i]
        sib6[i].wait_recv()
        p6sum[i] += p6sib[i]
        first = 1 if h == 0 else 2
        if q == 3:
            got[("f", h)] = send(p6sum.at[i], r6f.at[h], first, 0)
        elif q == first:
            got[("x", h)] = send(p6sum.at[i], r6x.at[h], first, 0)

    red2 = None
    for i, (q, h) in enumerate(units):
        p6out[i] = part6_of(q, h, 1)
        sib6[i] = send(p6out.at[i], p6sib.at[i], 0, 1)
        p6sum[i] = part6_of(q, h, 0)
        if i:
            fin6(i - 1)
        if i == 3:
            red2 = reduce_start(part2, rb2)
    fin6(len(units) - 1)
    for h, i in ((0, 4), (1, 5)):
        got[("f", h)].wait_recv()
        p6sum[i] += r6f[h]
        got[("y", h)] = send(p6sum.at[i], r6y.at[h], 2 if h == 0 else 1, 0)
    out2 = reduce_mid(part2, rb2, res2, red2)
    for h in (0, 1):
        got[("x", h)].wait_recv()
        p6sum[6 + h] += r6x[h]
    for cp in out2:
        cp.wait_recv()
    o2_ref[...] = res2[...]
    acc = None
    for h in (0, 1):
        got[("y", h)].wait_recv()
        d1[h] = (p6sum[6 + h] + r6y[h]).astype(BF16)
        term = dot(d1[h], xg[0, h * half:(h + 1) * half, :])
        acc = term if acc is None else acc + term
    part1[...] = acc
    red1 = reduce_start(part1, rb1)
    out1 = reduce_mid(part1, rb1, res1, red1)
    for cp in out1:
        cp.wait_recv()
    o1_ref[...] = res1[...]
    for cp in sent:
        cp.wait_send()


def solution(mesh):
    def local_step(adj_rows, features, w_one, w_two, labels, label_mask):
        nb, f_in = features.shape
        total = adj_rows.shape[1]
        hid, classes = w_two.shape
        cpad = 48
        lanes = 128
        xp = jnp.concatenate([features, label_mask[:, None].astype(BF16), jnp.zeros((nb, lanes - f_in - 1), BF16)], axis=1)
        w1p = jnp.pad(w_one.astype(BF16), ((0, lanes - f_in), (0, 0)))
        w2p = jnp.pad(w_two.astype(BF16), ((0, 0), (0, cpad - classes)))
        vmem = pl.BlockSpec(memory_space=pltpu.VMEM)
        anyspec = pl.BlockSpec(memory_space=pl.ANY)
        V = pltpu.VMEM
        nsem = 160
        half = nb // 2
        o1, o2 = pl.pallas_call(
            functools.partial(step_kernel, nb, classes, f_in, cpad),
            out_shape=[jax.ShapeDtypeStruct((hid, lanes), F32), jax.ShapeDtypeStruct((hid, lanes), F32)],
            in_specs=[anyspec, anyspec, vmem, vmem, vmem, vmem, vmem],
            out_specs=[vmem, vmem],
            scratch_shapes=[
                V((total // nb, nb, nb), BF16), V((16, nb, lanes), BF16), V((nb, hid), BF16), V((16, lanes), F32),
                V((nb, hid), F32), V((2, hid, nb), BF16), V((16, cpad, nb), BF16), V((nb, lanes), F32), V((2, cpad, nb), BF16),
                V((4, cpad, nb), F32), V((4, cpad, nb), F32), V((4, cpad, nb), F32), V((3, cpad, nb), F32),
                V((2, cpad, nb), BF16), V((2, hid, nb), BF16),
                V((8, hid, half), F32), V((8, hid, half), F32), V((8, hid, half), F32),
                V((2, hid, half), F32), V((2, hid, half), F32), V((2, hid, half), F32), V((2, hid, half), BF16),
                V((hid, lanes), F32), V((hid, lanes), F32), V((15, hid // 16, lanes), F32), V((15, hid // 16, lanes), F32),
                V((hid, lanes), F32), V((hid, lanes), F32),
                pltpu.SemaphoreType.DMA((16,)), pltpu.SemaphoreType.DMA,
                pltpu.SemaphoreType.DMA((nsem,)), pltpu.SemaphoreType.DMA((nsem,)),
            ],
            compiler_params=pltpu.CompilerParams(collective_id=0, has_side_effects=True, vmem_limit_bytes=67043328),
            name="gcn_step",
        )(adj_rows, xp, w1p, w2p, w2p.T, labels.reshape(1, nb), label_mask.reshape(1, nb))
        return o2[0, classes], o1[:, :f_in].T, o2[:, :classes]

    row_spec = P(("nodes", "rep"))
    return jax.shard_map(local_step, mesh=mesh, in_specs=(P("nodes", None), P(("nodes", "rep"), None), P(), P(), row_spec, row_spec), out_specs=(P(), P(), P()), check_vma=False)
```

time: 605 us -> 158 us (0.26)
  local copies, waits for them, and re-layouts: 227 us -> 7.96 us
  waiting for transfers between devices: 194 us -> 0 us
  Pallas kernels: 0 us -> 146 us
  blocking collectives: 80.7 us -> 0 us
  matrix products: 75.6 us -> 0 us
  between operations: 17.4 us -> 0.67 us
    pallas_call x0 -> x1, Pallas kernels: none -> 146 us  [local_step(): pl.pallas_call(functools.partial(step_kernel, nb, classes, f_in, cpad), o...]
    reduce_scatter x4 -> x0, waiting for transfers between devices: 140 us -> none  [the longest x2 96.9 us: aggregate_t(): lax.psum_scatter(partial_sum, 'nodes', scatter_dimension=0, tiled=False)]
    reshape x1 -> x0, local copies, waits for them, and re-layouts: 107 us -> none  [local_step(): adj_split = adj_rows.reshape(group_rows_n, node_size, rep_size, rows_dev)]
    dynamic_slice x1 -> x0, local copies, waits for them, and re-layouts: 82.4 us -> none  [local_step(): lax.dynamic_index_in_dim(adj_split, lax.axis_index('rep'), axis=2, keepdi...]
    dot_general x9 -> x0, matrix products: 75.6 us -> none  [the longest x2 34 us: aggregate(): jnp.einsum('ajb,jbf->af', adj_mine, gathered, preferred_element_type=jnp....]
    psum x2 -> x0, blocking collectives: 64.8 us -> none  [the longest x1 32.8 us: local_step(): lax.psum(jnp.einsum('vh,vc->hc', h_one, dy_two, preferred_element_type=jn...]
    psum x1 -> x0, waiting for transfers between devices: 34.7 us -> none  [local_step(): lax.psum(jnp.einsum('vf,vh->fh', features, dy_one, preferred_element_type...]
    unnamed x15 -> x4, local copies, waits for them, and re-layouts: 36.9 us -> 3.61 us
  transfers between devices with their start and end apart: 7 -> 0, of which waited for: 6 -> 0; matrix products, arithmetic and copies ran while one was open for 37% -> 0% of each run, Pallas kernels for 0% -> 0%
where the time goes in v1:
time: 158 us
  Pallas kernels  146 us (92%)
  local copies, waits for them, and re-layouts  7.96 us (5%)
  other arithmetic  3.25 us (2%)
    pallas_call x1, Pallas kernels, local_step(): pl.pallas_call(functools.partial(step_kernel, nb, classes, f_in, cpad), o...  146 us
    unnamed x4, local copies, waits for them, and re-layouts  3.61 us

profile of v1, /device:TPU:0, one launch (start us, length us, event | category | flops | bytes accessed | tf_op | source)
XLA Modules:
  0.0 157.9 jit_solution(11445957428036060324)
XLA Ops:
  0.6 0.7 convert_element_type.16
  1.3 0.2 convert_element_type.20
  1.5 1.1 copy.13
  2.7 0.1 pad.12.clone
  2.7 0.9 maximum_maximum_fusion.x_hbm
  3.6 0.9 convert_element_type.18
  4.5 0.6 pad.8.w1_ref
  5.1 0.8 convert_element_type.19
  5.9 0.1 copy.18
  6.1 0.7 pad.9.clone.w2_ref
  6.7 0.6 pad_bitcast_fusion.w2t_ref
  7.3 146.0 %gcn_step.1 = (f32[256,128]{1,0:T(8,128)}, f32[256,128]{1,0:T(8,128)}) custom-call(bf16[2048,16384]{1,0:T(8,128)(2,1)} %a_hbm.1, bf16[1024,128]{1,0:T(8,128)(2,1)} %maximum_maximum_fusion.x_hbm, bf16[128,256]{1,0:T(8,128)(2,1)} %pad.8.w1_ref, bf16[256,48]{1,0:T(8,128)(2,1)} %pad.9.clone.w2_ref, bf16[48,256]{1,0:T(8,128)(2,1)} %pad_bitcast_fusion.w2t_ref, ...), custom_call_target="tpu_custom_call" | custom-call | tf_op jit(solution)/shard_map/gcn_step/pallas_call | solution.py:305
  153.3 1.3 slice.9
  154.6 0.9 slice_bitcast_fusion
  155.5 0.7 copy.16
  156.2 1.6 %copy.17 = f32[256,47]{0,1:T(8,128)} copy(f32[256,47]{1,0:T(8,128)} %bitcast.8) | data formatting | bytes 96256
  (1 shorter events, 0.0 us)

commit v2 on v1

--- a/solution.py
+++ b/solution.py
@@ -8,6 +8,7 @@
 from jax.sharding import PartitionSpec as P
 
 BF16 = jnp.bfloat16
+scope = jax.named_scope
 F32 = jnp.float32
 
 POS = {0: 0, 1: 1, 2: 2, 4: 3, 3: 4, 5: 5, 6: 6, 7: 7}
@@ -60,23 +61,24 @@
 
     xload = pltpu.make_async_copy(x_hbm, xg.at[0], xsem)
     xload.start()
-    loads = {}
-    for k in POS:
-        for dc in range(2):
-            slot = POS[k] * 2 + dc
-            col = pl.multiple_of(block_id(k, dc) * nb, nb)
-            row = pl.multiple_of(r * nb, nb)
-            cp = pltpu.make_async_copy(a_hbm.at[pl.ds(row, nb), pl.ds(col, nb)], abuf.at[slot], asem.at[slot])
-            cp.start()
-            loads[slot] = cp
     barrier = pltpu.get_barrier_semaphore()
     for k, dc in peers:
         pl.semaphore_signal(barrier, inc=1, device_id=coords(k, dc), device_id_type=pl.DeviceIdType.MESH)
     cnt[...] = jnp.zeros_like(cnt)
     z1[...] = jnp.zeros_like(z1)
     z2[...] = jnp.zeros_like(z2)
-    pl.semaphore_wait(barrier, len(peers))
-    xload.wait()
+    with scope("entry"):
+        xload.wait()
+        loads = {}
+        for k in POS:
+            for dc in range(2):
+                slot = POS[k] * 2 + dc
+                col = pl.multiple_of(block_id(k, dc) * nb, nb)
+                row = pl.multiple_of(r * nb, nb)
+                cp = pltpu.make_async_copy(a_hbm.at[pl.ds(row, nb), pl.ds(col, nb)], abuf.at[slot], asem.at[slot])
+                cp.start()
+                loads[slot] = cp
+        pl.semaphore_wait(barrier, len(peers))
 
     def gather(buf, cuts, consume):
         def at(k, dc):
@@ -87,11 +89,13 @@
 
         near = {k: send(at(0, 0), at(k, 0), k, 0) for k in (1, 2, 4)}
         sib = {0: send(at(0, 0), at(0, 1), 0, 1)}
-        sib[0].wait_recv()
-        consume(0, 2)
+        with scope("g0"):
+            sib[0].wait_recv()
+            consume(0, 2)
         two = {}
         for k in (1, 2, 4):
-            near[k].wait_recv()
+            with scope("g1_wait"):
+                near[k].wait_recv()
             for p, (d0, d1_, d2_) in enumerate(ORDERS):
                 if k == d0:
                     two[(d0 + d1_, p)] = send(piece(d0, p), piece(d0 + d1_, p), d1_, 0)
@@ -99,24 +103,32 @@
                 if k == d1_:
                     two[(d1_ + d2_, p)] = send(piece(d1_, p), piece(d1_ + d2_, p), d2_, 0)
             sib[k] = send(at(k, 0), at(k, 1), 0, 1)
-        for k in (1, 2, 4):
-            sib[k].wait_recv()
-        consume(2, 8)
+        with scope("g1_sib"):
+            for k in (1, 2, 4):
+                sib[k].wait_recv()
+        with scope("g1_compute"):
+            consume(2, 8)
         three = []
         for k in (3, 6, 5):
             for p, (d0, d1_, d2_) in enumerate(ORDERS):
-                two[(k, p)].wait_recv()
+                with scope("g2_wait"):
+                    two[(k, p)].wait_recv()
                 if k == d0 + d1_:
                     three.append(send(piece(k, p), piece(7, p), d2_, 0))
             sib[k] = send(at(k, 0), at(k, 1), 0, 1)
-        for k in (3, 6, 5):
-            sib[k].wait_recv()
-        consume(8, 14)
-        for cp in three:
-            cp.wait_recv()
+        with scope("g2_sib"):
+            for k in (3, 6, 5):
+                sib[k].wait_recv()
+        with scope("g2_compute"):
+            consume(8, 14)
+        with scope("g3_wait"):
+            for cp in three:
+                cp.wait_recv()
         sib[7] = send(at(7, 0), at(7, 1), 0, 1)
-        sib[7].wait_recv()
-        consume(14, 16)
+        with scope("g3_sib"):
+            sib[7].wait_recv()
+        with scope("g3_compute"):
+            consume(14, 16)
 
     ones = jnp.ones((16, nb), BF16)
     mrows = 256
@@ -137,9 +149,10 @@
     third = (nb // 48) * 16
     gather(xg, (0, nb - 2 * third, nb - third, nb), z1_blocks)
 
-    for m in range(0, nb, mrows):
-        h1t[0, :, m:m + mrows] = jnp.maximum(z1[m:m + mrows, :], 0.0).T.astype(BF16)
-    y2g[0] = dot(w2t_ref[...], h1t[0]).astype(BF16)
+    with scope("h1y2"):
+        for m in range(0, nb, mrows):
+            h1t[0, :, m:m + mrows] = jnp.maximum(z1[m:m + mrows, :], 0.0).T.astype(BF16)
+        y2g[0] = dot(w2t_ref[...], h1t[0]).astype(BF16)
 
     reload = {}
 
@@ -161,7 +174,6 @@
 
     third = cpad // 3
     gather(y2g, (0, third, 2 * third, cpad), z2_blocks)
-    h1t_cp = send(h1t.at[0], h1t.at[1], 4, 0)
 
     z2t = z2[...].T[0:cpad, :]
     cls = lax.broadcasted_iota(jnp.int32, (cpad, nb), 0)
@@ -175,15 +187,18 @@
     loss_part = jnp.sum(loss_v, axis=1, keepdims=True) / total_m
     g2[0] = ((jnp.exp(logp) - hot.astype(F32)) * (mask_f / total_m)).astype(BF16)
     g2_cp = send(g2.at[0], g2.at[1], 4, 0)
-    g2_cp.wait_recv()
-    for s in reload:
-        reload[s].wait()
+    h1t_cp = send(h1t.at[0], h1t.at[1], 4, 0)
+    with scope("g2z_wait"):
+        g2_cp.wait_recv()
+        for s in reload:
+            reload[s].wait()
 
     order = (3, 1, 2, 0)
     sib2, rcv2 = {}, {}
 
     def fin2(q):
-        sib2[q].wait_recv()
+        with scope("p2sib"):
+            sib2[q].wait_recv()
         p2sum[q] += p2sib[q]
         if q:
             rcv2[q] = send(p2sum.at[q], p2rcv.at[q - 1], q, 0)
@@ -193,14 +208,17 @@
         return dot(g2[0], abuf[s]) + dot(g2[1], abuf[sp])
 
     for i, q in enumerate(order):
-        p2out[q] = part2_of(q, 1)
+        with scope("p2a"):
+            p2out[q] = part2_of(q, 1)
         sib2[q] = send(p2out.at[q], p2sib.at[q], 0, 1)
-        p2sum[q] = part2_of(q, 0)
+        with scope("p2b"):
+            p2sum[q] = part2_of(q, 0)
         if i:
             fin2(order[i - 1])
     fin2(0)
-    for q in (1, 2, 3):
-        rcv2[q].wait_recv()
+    with scope("p2rcv"):
+        for q in (1, 2, 3):
+            rcv2[q].wait_recv()
     d2[0] = (p2sum[0] + p2rcv[0] + p2rcv[1] + p2rcv[2]).astype(BF16)
     d2_cp = send(d2.at[0], d2.at[1], 4, 0)
 
@@ -222,14 +240,17 @@
     def g1_of(i):
         g1[i] = jnp.where(h1t[i] > 0, dot(w2_ref[...], d2[i]), 0.0).astype(BF16)
 
-    g1_of(0)
     lane = lax.broadcasted_iota(jnp.int32, (hid, cpad), 1)
     dw2 = dot(h1t[0], d2[0], ((1,), (1,)))
     part2[...] = jnp.zeros_like(part2)
     part2[:, 0:cpad] = jnp.where(lane == classes, loss_part, dw2)
+    red2 = reduce_start(part2, rb2)
+    g1_of(0)
     h1t_cp.wait_recv()
-    d2_cp.wait_recv()
-    g1_of(1)
+    with scope("d2z_wait"):
+        d2_cp.wait_recv()
+    with scope("g1b"):
+        g1_of(1)
 
     half = nb // 2
     units = ((3, 0), (3, 1), (1, 0), (2, 1), (2, 0), (1, 1), (0, 0), (0, 1))
@@ -242,7 +263,8 @@
 
     def fin6(i):
         q, h = units[i]
-        sib6[i].wait_recv()
+        with scope("p6sib"):
+            sib6[i].wait_recv()
         p6sum[i] += p6sib[i]
         first = 1 if h == 0 else 2
         if q == 3:
@@ -250,41 +272,48 @@
         elif q == first:
             got[("x", h)] = send(p6sum.at[i], r6x.at[h], first, 0)
 
-    red2 = None
     for i, (q, h) in enumerate(units):
-        p6out[i] = part6_of(q, h, 1)
+        with scope("p6a"):
+            p6out[i] = part6_of(q, h, 1)
         sib6[i] = send(p6out.at[i], p6sib.at[i], 0, 1)
-        p6sum[i] = part6_of(q, h, 0)
+        with scope("p6b"):
+            p6sum[i] = part6_of(q, h, 0)
         if i:
             fin6(i - 1)
-        if i == 3:
-            red2 = reduce_start(part2, rb2)
+        if i == 1:
+            out2 = reduce_mid(part2, rb2, res2, red2)
     fin6(len(units) - 1)
     for h, i in ((0, 4), (1, 5)):
-        got[("f", h)].wait_recv()
+        with scope("f_wait"):
+            got[("f", h)].wait_recv()
         p6sum[i] += r6f[h]
         got[("y", h)] = send(p6sum.at[i], r6y.at[h], 2 if h == 0 else 1, 0)
-    out2 = reduce_mid(part2, rb2, res2, red2)
     for h in (0, 1):
-        got[("x", h)].wait_recv()
+        with scope("x_wait"):
+            got[("x", h)].wait_recv()
         p6sum[6 + h] += r6x[h]
-    for cp in out2:
-        cp.wait_recv()
+    with scope("out2_wait"):
+        for cp in out2:
+            cp.wait_recv()
     o2_ref[...] = res2[...]
     acc = None
     for h in (0, 1):
-        got[("y", h)].wait_recv()
+        with scope("y_wait"):
+            got[("y", h)].wait_recv()
         d1[h] = (p6sum[6 + h] + r6y[h]).astype(BF16)
         term = dot(d1[h], xg[0, h * half:(h + 1) * half, :])
         acc = term if acc is None else acc + term
     part1[...] = acc
-    red1 = reduce_start(part1, rb1)
-    out1 = reduce_mid(part1, rb1, res1, red1)
-    for cp in out1:
-        cp.wait_recv()
+    with scope("red1"):
+        red1 = reduce_start(part1, rb1)
+        out1 = reduce_mid(part1, rb1, res1, red1)
+    with scope("out1_wait"):
+        for cp in out1:
+            cp.wait_recv()
     o1_ref[...] = res1[...]
-    for cp in sent:
-        cp.wait_send()
+    with scope("send_wait"):
+        for cp in sent:
+            cp.wait_send()
 
 
 def solution(mesh):

time: 158 us -> 138 us (0.87)
  Pallas kernels: 146 us -> 126 us
    pallas_call x1, Pallas kernels: 146 us -> 126 us  [local_step(): pl.pallas_call(functools.partial(step_kernel, nb, classes, f_in, cpad), o...]
where the time goes in v2:
time: 138 us
  Pallas kernels  126 us (91%)
  local copies, waits for them, and re-layouts  7.96 us (6%)
  other arithmetic  3.25 us (2%)
    pallas_call x1, Pallas kernels, local_step(): pl.pallas_call(functools.partial(step_kernel, nb, classes, f_in, cpad), o...  126 us
    unnamed x4, local copies, waits for them, and re-layouts  3.61 us

profile of v2, /device:TPU:0, one launch (start us, length us, event | category | flops | bytes accessed | tf_op | source)
XLA Modules:
  0.0 137.8 jit_solution(16032283215547600507)
XLA Ops:
  0.6 0.7 convert_element_type.16
  1.3 0.2 convert_element_type.20
  1.5 1.1 copy.13
  2.7 0.1 pad.12.clone
  2.7 0.9 maximum_maximum_fusion.x_hbm
  3.6 0.9 convert_element_type.18
  4.5 0.6 pad.8.w1_ref
  5.1 0.8 convert_element_type.19
  5.9 0.1 copy.18
  6.1 0.7 pad.9.clone.w2_ref
  6.7 0.6 pad_bitcast_fusion.w2t_ref
  7.3 125.9 %gcn_step.1 = (f32[256,128]{1,0:T(8,128)}, f32[256,128]{1,0:T(8,128)}) custom-call(bf16[2048,16384]{1,0:T(8,128)(2,1)} %a_hbm.1, bf16[1024,128]{1,0:T(8,128)(2,1)} %maximum_maximum_fusion.x_hbm, bf16[128,256]{1,0:T(8,128)(2,1)} %pad.8.w1_ref, bf16[256,48]{1,0:T(8,128)(2,1)} %pad.9.clone.w2_ref, bf16[48,256]{1,0:T(8,128)(2,1)} %pad_bitcast_fusion.w2t_ref, ...), custom_call_target="tpu_custom_call" | custom-call | tf_op jit(solution)/shard_map/gcn_step/pallas_call | solution.py:334
  133.3 1.3 slice.9
  134.5 0.9 slice_bitcast_fusion
  135.4 0.7 copy.16
  136.2 1.6 %copy.17 = f32[256,47]{0,1:T(8,128)} copy(f32[256,47]{1,0:T(8,128)} %bitcast.8) | data formatting | bytes 96256
  (1 shorter events, 0.0 us)

commit v3 on v2

v3 whole, which is shorter than its diff:
```python
import functools

import jax
import jax.numpy as jnp
from jax import lax
from jax.experimental import pallas as pl
from jax.experimental.pallas import tpu as pltpu
from jax.sharding import PartitionSpec as P

BF16 = jnp.bfloat16
F32 = jnp.float32
scope = jax.named_scope

SLOTS = {(0, 0): 0, (0, 1): 1, (1, 0): 2, (2, 0): 3, (4, 0): 4, (1, 1): 5, (2, 1): 6, (4, 1): 7,
         (3, 0): 8, (6, 0): 9, (5, 0): 10, (3, 1): 11, (6, 1): 12, (5, 1): 13, (7, 0): 14, (7, 1): 15}
ORDERS = ((1, 2, 4), (2, 4, 1), (4, 1, 2))
COUNT_BASE = 32.0


def dot(a, b, dims=((1,), (0,))):
    return lax.dot_general(a, b, (dims, ((), ())), preferred_element_type=F32)


def step_kernel(nb, classes, f_in, cpad,
                a_hbm, x_hbm, w1_hbm, w2_hbm, lab_hbm, msk_hbm,
                loss_ref, o1_ref, o2_ref,
                abuf, xg, y1, z1, h1t, y2g, z2, g2,
                xraw, w1raw, w2raw, lab_ref, msk_ref, w1t_ref, w2_ref, w2t_ref, w1f, w2f,
                p2out, p2sib, p2sum, p2rcv, d2, g1,
                p6out, p6sib, p6sum, r6f, r6x, r6y, d1,
                part1, part2, rb1, rb2, res1, res2,
                asem, psem, ssem, rsem):
    r = lax.axis_index("rep")
    n = lax.axis_index("nodes")
    core = n % 2
    xc = (n // 2) % 2
    yc = n // 4
    hid = z1.shape[1]
    fpad = xg.shape[1]

    def flip(v, f):
        return 1 - v if f else v

    def coords(k, dc):
        rr = flip(r, k // 4)
        nn = flip(yc, (k // 2) % 2) * 4 + flip(xc, k % 2) * 2 + flip(core, dc)
        return rr, nn

    def block_id(k, dc):
        rr, nn = coords(k, dc)
        return nn * 2 + rr

    sent = []

    def prepare(src, dst, k, dc):
        i = len(sent)
        cp = pltpu.make_async_remote_copy(
            src_ref=src, dst_ref=dst, send_sem=ssem.at[i], recv_sem=rsem.at[i],
            device_id=coords(k, dc), device_id_type=pl.DeviceIdType.MESH)
        sent.append(cp)
        return cp

    def send(src, dst, k, dc):
        cp = prepare(src, dst, k, dc)
        cp.start()
        return cp

    peers = [(k, dc) for k in range(8) for dc in range(2) if (k, dc) != (0, 0)]

    pre = [pltpu.make_async_copy(src, dst, psem.at[i]) for i, (src, dst) in enumerate(
        ((x_hbm, xraw), (msk_hbm, msk_ref), (w1_hbm, w1raw), (w2_hbm, w2raw), (lab_hbm, lab_ref)))]
    for cp in pre:
        cp.start()
    barrier = pltpu.get_barrier_semaphore()
    for k, dc in peers:
        pl.semaphore_signal(barrier, inc=1, device_id=coords(k, dc), device_id_type=pl.DeviceIdType.MESH)
    z1[...] = jnp.zeros_like(z1)
    z2[...] = jnp.zeros_like(z2)
    part1[...] = jnp.zeros_like(part1)
    part2[...] = jnp.zeros_like(part2)
    w1f[...] = jnp.zeros_like(w1f)
    w2f[...] = jnp.zeros_like(w2f)
    xg[0] = jnp.zeros((fpad, nb), BF16)
    with scope("entry_x"):
        pre[0].wait()
        pre[1].wait()

    def a_rows(group_row, k, dc, slot):
        row = pl.multiple_of(group_row * nb, nb)
        col = pl.multiple_of(block_id(k, dc) * nb, nb)
        return pltpu.make_async_copy(a_hbm.at[pl.ds(row, nb), pl.ds(col, nb)], abuf.at[slot], asem.at[slot])

    for (k, dc), slot in SLOTS.items():
        a_rows(r, k, dc, slot).start()

    xg[0, 0:f_in, :] = xraw[...]
    count = jnp.sum(msk_ref[...].astype(F32), axis=1, keepdims=True)
    hi = jnp.floor(count * (1.0 / COUNT_BASE))
    lo = count - COUNT_BASE * hi
    row16 = lax.broadcasted_iota(jnp.int32, (16, 128), 0) + (fpad - 16)
    tail = xg[0, fpad - 16:fpad, 0:128].astype(F32)
    tail = jnp.where(row16 == f_in, hi, jnp.where(row16 == f_in + 1, lo, tail))
    xg[0, fpad - 16:fpad, 0:128] = tail.astype(BF16)
    with scope("entry_w"):
        for cp in pre[2:]:
            cp.wait()
    w1f[0:f_in, :] = w1raw[...]
    w1t_ref[...] = w1f[...].T[:, 0:fpad].astype(BF16)
    w2f[0:classes, :] = w2raw[...]
    w2t_ref[...] = w2f[0:cpad, :].astype(BF16)
    w2_ref[...] = w2f[...].T[:, 0:cpad].astype(BF16)
    with scope("entry_barrier"):
        pl.semaphore_wait(barrier, len(peers))

    def gather(buf, cuts, by_node, pair_work, after_pair):
        def at(k, dc):
            return buf.at[SLOTS[k, dc]]

        def piece(k, p):
            span = pl.ds(cuts[p], cuts[p + 1] - cuts[p])
            return buf.at[(SLOTS[k, 0], slice(None), span) if by_node else (SLOTS[k, 0], span)]

        sib0 = send(at(0, 0), at(0, 1), 0, 1)
        near, two, three, sib = {}, {}, {}, {0: sib0}
        for j in range(3):
            for p, order in enumerate(ORDERS):
                near[j, p] = send(piece(0, p), piece(order[j], p), order[j], 0)
        for p, (d0, d1_, d2_) in enumerate(ORDERS):
            two[0, p] = prepare(piece(d0, p), piece(d0 + d1_, p), d1_, 0)
            two[1, p] = prepare(piece(d0, p), piece(d0 + d2_, p), d2_, 0)
            two[2, p] = prepare(piece(d1_, p), piece(d1_ + d2_, p), d2_, 0)
            three[p] = prepare(piece(d0 + d1_, p), piece(7, p), d2_, 0)
        for k in range(1, 8):
            sib[k] = prepare(at(k, 0), at(k, 1), 0, 1)

        def wait(*cps):
            for cp in cps:
                cp.wait_recv()

        def start(*cps):
            for cp in cps:
                cp.start()

        def event(t):
            if t == 0:
                wait(sib[0])
            if t == 1:
                for p in range(3):
                    wait(near[0, p])
                    start(two[0, p], two[1, p])
                for p in range(3):
                    wait(near[1, p])
                    start(two[2, p])
                for p in range(3):
                    wait(near[2, p])
                start(sib[1], sib[2], sib[4])
            if t == 2:
                for p in range(3):
                    wait(two[0, p])
                    start(three[p])
                wait(sib[1])
            if t == 3:
                wait(sib[2], sib[4])
            if t == 4:
                for p in range(3):
                    wait(two[1, p], two[2, p])
                start(sib[3], sib[6], sib[5])
            if t == 5:
                wait(sib[3])
            if t == 6:
                for p in range(3):
                    wait(three[p])
                start(sib[7])
                wait(sib[6], sib[5])
            if t == 7:
                wait(sib[7])

        @pl.loop(0, 8)
        def _(t):
            for u in range(8):
                @pl.when(t == u)
                def _():
                    with scope(f"ev{u}"):
                        event(u)
                        if u:
                            after_pair(u - 1)
            with scope("pair"):
                pair_work(t)
        after_pair(7)

    mrows = nb // 2

    def z1_pair(t):
        for j in range(2):
            s = 2 * t + j
            pltpu.make_async_copy(a_hbm.at[pl.ds(0, nb), pl.ds(0, nb)], abuf.at[s], asem.at[s]).wait()
            y1[j] = dot(w1t_ref[...], xg[s]).astype(BF16)
        for m in range(0, nb, mrows):
            z1[m:m + mrows, :] += (dot(abuf[2 * t, m:m + mrows, :], y1[0], ((1,), (1,)))
                                   + dot(abuf[2 * t + 1, m:m + mrows, :], y1[1], ((1,), (1,))))

    third = (nb // 3 // 128 + 1) * 128
    gather(xg, (0, third, 2 * third, nb), True, z1_pair, lambda t: None)

    with scope("h1y2"):
        for m in range(0, nb, 256):
            h1t[0, :, m:m + 256] = jnp.maximum(z1[m:m + 256, :], 0.0).T.astype(BF16)
        y2g[0] = dot(w2t_ref[...], h1t[0]).astype(BF16)

    def z2_pair(t):
        for m in range(0, nb, mrows):
            z2[m:m + mrows, 0:cpad] += (dot(abuf[2 * t, m:m + mrows, :], y2g[2 * t], ((1,), (1,)))
                                        + dot(abuf[2 * t + 1, m:m + mrows, :], y2g[2 * t + 1], ((1,), (1,))))

    def z2_after(t):
        for (k, dc), slot in SLOTS.items():
            if slot // 2 == t and k >= 4:
                a_rows(1 - r, k - 4, dc, slot).start()

    third = cpad // 3
    gather(y2g, (0, third, 2 * third, cpad), False, z2_pair, z2_after)

    tails = xg[0, fpad - 16:fpad, 0:128].astype(F32)
    for s in range(1, 16):
        tails = tails + xg[s, fpad - 16:fpad, 0:128].astype(F32)
    at_hi = f_in - (fpad - 16)
    total_m = COUNT_BASE * tails[at_hi:at_hi + 1, 0:1] + tails[at_hi + 1:at_hi + 2, 0:1]
    z2t = z2[...].T[0:cpad, :]
    cls = lax.broadcasted_iota(jnp.int32, (cpad, nb), 0)
    zm = jnp.where(cls < classes, z2t, -jnp.inf)
    zs = zm - jnp.max(zm, axis=0, keepdims=True)
    logp = zs - jnp.log(jnp.sum(jnp.exp(zs), axis=0, keepdims=True))
    hot = cls == lab_ref[...]
    mask_f = msk_ref[...].astype(F32)
    loss_v = -mask_f * jnp.sum(jnp.where(hot, logp, 0.0), axis=0, keepdims=True)
    loss_part = jnp.sum(loss_v, axis=1, keepdims=True) / total_m
    g2[0] = ((jnp.exp(logp) - hot.astype(F32)) * (mask_f / total_m)).astype(BF16)
    g2_cp = send(g2.at[0], g2.at[1], 4, 0)
    h1t_cp = send(h1t.at[0], h1t.at[1], 4, 0)

    order = (3, 1, 2, 0)
    sib2, rcv2 = {}, {}

    with scope("p2own"):
        for q in order:
            p2out[q] = dot(g2[0], abuf[SLOTS[q, 1]])
            p2sum[q] = dot(g2[0], abuf[SLOTS[q, 0]])
    with scope("g2z_wait"):
        g2_cp.wait_recv()
        for (k, dc), slot in SLOTS.items():
            if k >= 4:
                a_rows(1 - r, k - 4, dc, slot).wait()

    def fin2(q):
        with scope("p2sib"):
            sib2[q].wait_recv()
        p2sum[q] += p2sib[q]
        if q:
            rcv2[q] = send(p2sum.at[q], p2rcv.at[q - 1], q, 0)

    for i, q in enumerate(order):
        with scope("p2a"):
            p2out[q] += dot(g2[1], abuf[SLOTS[q + 4, 1]])
        sib2[q] = send(p2out.at[q], p2sib.at[q], 0, 1)
        with scope("p2b"):
            p2sum[q] += dot(g2[1], abuf[SLOTS[q + 4, 0]])
        if i:
            fin2(order[i - 1])
    fin2(0)
    with scope("p2rcv"):
        for q in (1, 2, 3):
            rcv2[q].wait_recv()
    d2[0] = (p2sum[0] + p2rcv[0] + p2rcv[1] + p2rcv[2]).astype(BF16)
    d2_cp = send(d2.at[0], d2.at[1], 4, 0)

    rows = hid // 16

    def reduce_start(part, rb):
        return [send(part.at[pl.ds(pl.multiple_of(block_id(k, dc) * rows, rows), rows)], rb.at[i], k, dc)
                for i, (k, dc) in enumerate(peers)]

    def reduce_mid(part, rb, res, cps):
        own = pl.ds(pl.multiple_of(block_id(0, 0) * rows, rows), rows)
        acc = part[own, :]
        for i, cp in enumerate(cps):
            cp.wait_recv()
            acc = acc + rb[i]
        res[own, :] = acc
        return [send(res.at[own], res.at[own], k, dc) for k, dc in peers]

    def g1_of(i):
        g1[i] = jnp.where(h1t[i] > 0, dot(w2_ref[...], d2[i]), 0.0).astype(BF16)

    lane = lax.broadcasted_iota(jnp.int32, (hid, cpad), 1)
    dw2 = dot(h1t[0], d2[0], ((1,), (1,)))
    part2[:, 0:cpad] = jnp.where(lane == classes, loss_part, dw2)
    red2 = reduce_start(part2, rb2)
    g1_of(0)

    half = nb // 2
    units = ((3, 0), (3, 1), (1, 0), (2, 1), (2, 0), (1, 1), (0, 0), (0, 1))
    early = 2
    sib6, got = {}, {}

    def own6(q, h, dc):
        return dot(g1[0], abuf[SLOTS[q, dc], :, h * half:(h + 1) * half])

    def partner6(q, h, dc):
        return dot(g1[1], abuf[SLOTS[q + 4, dc], :, h * half:(h + 1) * half])

    def fin6(i):
        q, h = units[i]
        with scope("p6sib"):
            sib6[i].wait_recv()
        p6sum[i] += p6sib[i]
        first = 1 if h == 0 else 2
        if q == 3:
            got["f", h] = send(p6sum.at[i], r6f.at[h], first, 0)
        elif q == first:
            got["x", h] = send(p6sum.at[i], r6x.at[h], first, 0)

    with scope("p6own"):
        for i in range(early):
            p6out[i] = own6(*units[i], 1)
            p6sum[i] = own6(*units[i], 0)
    with scope("d2z_wait"):
        h1t_cp.wait_recv()
        d2_cp.wait_recv()
    with scope("g1b"):
        g1_of(1)
    with scope("p6early"):
        for i in range(early):
            p6out[i] += partner6(*units[i], 1)
            sib6[i] = send(p6out.at[i], p6sib.at[i], 0, 1)
        for i in range(early):
            p6sum[i] += partner6(*units[i], 0)
    for i in range(early):
        fin6(i)
    for i in range(early, len(units)):
        q, h = units[i]
        with scope("p6a"):
            p6out[i] = own6(q, h, 1) + partner6(q, h, 1)
        sib6[i] = send(p6out.at[i], p6sib.at[i], 0, 1)
        with scope("p6b"):
            p6sum[i] = own6(q, h, 0) + partner6(q, h, 0)
        if i > early:
            fin6(i - 1)
        if i == early:
            with scope("red2"):
                out2 = reduce_mid(part2, rb2, res2, red2)
    fin6(len(units) - 1)
    for h, i in ((0, 4), (1, 5)):
        with scope("f_wait"):
            got["f", h].wait_recv()
        p6sum[i] += r6f[h]
        got["y", h] = send(p6sum.at[i], r6y.at[h], 2 if h == 0 else 1, 0)
    for h in (0, 1):
        with scope("x_wait"):
            got["x", h].wait_recv()
        p6sum[6 + h] += r6x[h]
    with scope("out2_wait"):
        for cp in out2:
            cp.wait_recv()
    o2_ref[...] = res2[...].T[0:classes, :]
    loss_ref[...] = res2[0:1, classes:classes + 1]
    acc = None
    for h in (0, 1):
        with scope("y_wait"):
            got["y", h].wait_recv()
        d1[h] = (p6sum[6 + h] + r6y[h]).astype(BF16)
        term = dot(d1[h], xg[0, :, h * half:(h + 1) * half], ((1,), (1,)))
        acc = term if acc is None else acc + term
    part1[:, 0:fpad] = acc
    with scope("red1"):
        red1 = reduce_start(part1, rb1)
        out1 = reduce_mid(part1, rb1, res1, red1)
    with scope("out1_wait"):
        for cp in out1:
            cp.wait_recv()
    o1_ref[...] = res1[...].T[0:f_in, :]
    with scope("send_wait"):
        for cp in sent:
            cp.wait_send()


def solution(mesh):
    def local_step(adj_rows, features, w_one, w_two, labels, label_mask):
        nb, f_in = features.shape
        total = adj_rows.shape[1]
        hid, classes = w_two.shape
        cpad = 48
        lanes = 128
        fpad = 112
        half = nb // 2
        nsem = 144
        vmem = pl.BlockSpec(memory_space=pltpu.VMEM)
        anyspec = pl.BlockSpec(memory_space=pl.ANY)
        V = pltpu.VMEM
        loss, dw1, dw2 = pl.pallas_call(
            functools.partial(step_kernel, nb, classes, f_in, cpad),
            out_shape=[jax.ShapeDtypeStruct((1, 1), F32), jax.ShapeDtypeStruct((f_in, hid), F32),
                       jax.ShapeDtypeStruct((classes, hid), F32)],
            in_specs=[anyspec] * 6,
            out_specs=[vmem] * 3,
            scratch_shapes=[
                V((total // nb, nb, nb), BF16), V((16, fpad, nb), BF16), V((2, hid, nb), BF16),
                V((nb, hid), F32), V((2, hid, nb), BF16), V((16, cpad, nb), BF16), V((nb, lanes), F32), V((2, cpad, nb), BF16),
                V((f_in, nb), BF16), V((f_in, hid), F32), V((classes, hid), F32), V((1, nb), jnp.int32), V((1, nb), jnp.int32),
                V((hid, fpad), BF16), V((hid, cpad), BF16), V((cpad, hid), BF16), V((lanes, hid), F32), V((lanes, hid), F32),
                V((4, cpad, nb), F32), V((4, cpad, nb), F32), V((4, cpad, nb), F32), V((3, cpad, nb), F32),
                V((2, cpad, nb), BF16), V((2, hid, nb), BF16),
                V((8, hid, half), F32), V((8, hid, half), F32), V((8, hid, half), F32),
                V((2, hid, half), F32), V((2, hid, half), F32), V((2, hid, half), F32), V((2, hid, half), BF16),
                V((hid, lanes), F32), V((hid, lanes), F32), V((15, hid // 16, lanes), F32), V((15, hid // 16, lanes), F32),
                V((hid, lanes), F32), V((hid, lanes), F32),
                pltpu.SemaphoreType.DMA((16,)), pltpu.SemaphoreType.DMA((5,)),
                pltpu.SemaphoreType.DMA((nsem,)), pltpu.SemaphoreType.DMA((nsem,)),
            ],
            compiler_params=pltpu.CompilerParams(collective_id=0, has_side_effects=True, vmem_limit_bytes=67043328),
            name="gcn_step",
        )(adj_rows, features.T, w_one, w_two.T, labels.reshape(1, nb), label_mask.reshape(1, nb))
        return loss.reshape(()), dw1, dw2.T

    row_spec = P(("nodes", "rep"))
    return jax.shard_map(local_step, mesh=mesh, in_specs=(P("nodes", None), P(("nodes", "rep"), None), P(), P(), row_spec, row_spec), out_specs=(P(), P(), P()), check_vma=False)
```

time: 138 us -> 123 us (0.89)
  Pallas kernels: 126 us -> 117 us
  local copies, waits for them, and re-layouts: 7.96 us -> 2.97 us
  other arithmetic: 3.25 us -> 0 us
  between operations: 0.67 us -> 2.4 us
    pallas_call x1, Pallas kernels: 126 us -> 117 us  [local_step(): pl.pallas_call(functools.partial(step_kernel, nb, classes, f_in, cpad), o...]
    convert_element_type x3 -> x0, other arithmetic: 2.4 us -> none  [the longest x1 0.9 us: local_step(): w1p = jnp.pad(w_one.astype(BF16), ((0, lanes - f_in), (0, 0)))]
    transpose x2 -> x0, local copies, waits for them, and re-layouts: 1.53 us -> none  [the longest x1 0.91 us: local_step(): return (o2[0, classes], o1[:, :f_in].T, o2[:, :classes])]
    unnamed x4 -> x2, local copies, waits for them, and re-layouts: 3.61 us -> 2.97 us
where the time goes in v3:
time: 123 us
  Pallas kernels  117 us (95%)
  local copies, waits for them, and re-layouts  2.97 us (2%)
  between operations  2.4 us (2%)
    pallas_call x1, Pallas kernels, local_step(): pl.pallas_call(functools.partial(step_kernel, nb, classes, f_in, cpad), o...  117 us
    unnamed x2, local copies, waits for them, and re-layouts  2.97 us

profile of v3, /device:TPU:0, one launch (start us, length us, event | category | flops | bytes accessed | tf_op | source)
XLA Modules:
  0.0 122.7 jit_solution(5534186976226667436)
XLA Ops:
  0.6 117.4 %gcn_step.1 = (f32[1,1]{1,0:T(1,128)}, f32[100,256]{1,0:T(8,128)}, f32[47,256]{1,0:T(8,128)}) custom-call(bf16[2048,16384]{1,0:T(8,128)(2,1)} %a_hbm.1, bf16[100,1024]{1,0:T(8,128)(2,1)} %bitcast.6, f32[100,256]{1,0:T(8,128)} %w1_hbm.1, f32[47,256]{1,0:T(8,128)} %bitcast.7, s32[1,1024]{1,0:T(1,128)} %bitcast.9, s32[1,1024]{1,0:T(1,128)} %bitcast.10), custom_call_target="tpu_custom_call" | custom-call | tf_op jit(solution)/shard_map/gcn_step/pallas_call | solution.py:399
  118.6 1.5 %copy.13 = f32[100,256]{1,0:T(8,128)} copy(f32[100,256]{1,0:T(8,128)} %get-tuple-element.13) | data formatting | bytes 204800
  120.2 1.4 %copy.14 = f32[256,47]{0,1:T(8,128)} copy(f32[256,47]{0,1:T(8,128)} %bitcast.8) | data formatting | bytes 96256

commit v4 on v3

--- a/solution.py
+++ b/solution.py
@@ -26,9 +26,9 @@
                 loss_ref, o1_ref, o2_ref,
                 abuf, xg, y1, z1, h1t, y2g, z2, g2,
                 xraw, w1raw, w2raw, lab_ref, msk_ref, w1t_ref, w2_ref, w2t_ref, w1f, w2f,
-                p2out, p2sib, p2sum, p2rcv, d2, g1,
-                p6out, p6sib, p6sum, r6f, r6x, r6y, d1,
-                part1, part2, rb1, rb2, res1, res2,
+                p2out, p2sib, p2sum, p2fwd, p2far, d2, g1,
+                p6out, p6sib, p6sum, p6fwd, p6far, d1,
+                part1, part2, rb1, rbc, rbz, sumc, sumz, res1, res2,
                 asem, psem, ssem, rsem):
     r = lax.axis_index("rep")
     n = lax.axis_index("nodes")
@@ -65,14 +65,15 @@
         cp.start()
         return cp
 
-    peers = [(k, dc) for k in range(8) for dc in range(2) if (k, dc) != (0, 0)]
+    peers = [(k, dc) for k in (7, 3, 5, 6, 1, 2, 4, 0) for dc in range(2) if (k, dc) != (0, 0)]
 
     pre = [pltpu.make_async_copy(src, dst, psem.at[i]) for i, (src, dst) in enumerate(
         ((x_hbm, xraw), (msk_hbm, msk_ref), (w1_hbm, w1raw), (w2_hbm, w2raw), (lab_hbm, lab_ref)))]
     for cp in pre:
         cp.start()
     barrier = pltpu.get_barrier_semaphore()
-    for k, dc in peers:
+    near_peers = ((0, 1), (1, 0), (2, 0), (4, 0))
+    for k, dc in near_peers:
         pl.semaphore_signal(barrier, inc=1, device_id=coords(k, dc), device_id_type=pl.DeviceIdType.MESH)
     z1[...] = jnp.zeros_like(z1)
     z2[...] = jnp.zeros_like(z2)
@@ -110,7 +111,7 @@
     w2t_ref[...] = w2f[0:cpad, :].astype(BF16)
     w2_ref[...] = w2f[...].T[:, 0:cpad].astype(BF16)
     with scope("entry_barrier"):
-        pl.semaphore_wait(barrier, len(peers))
+        pl.semaphore_wait(barrier, len(near_peers))
 
     def gather(buf, cuts, by_node, pair_work, after_pair):
         def at(k, dc):
@@ -155,11 +156,11 @@
                     wait(near[2, p])
                 start(sib[1], sib[2], sib[4])
             if t == 2:
+                wait(sib[1])
+            if t == 3:
                 for p in range(3):
                     wait(two[0, p])
                     start(three[p])
-                wait(sib[1])
-            if t == 3:
                 wait(sib[2], sib[4])
             if t == 4:
                 for p in range(3):
@@ -194,6 +195,8 @@
         for j in range(2):
             s = 2 * t + j
             pltpu.make_async_copy(a_hbm.at[pl.ds(0, nb), pl.ds(0, nb)], abuf.at[s], asem.at[s]).wait()
+        for j in range(2):
+            s = 2 * t + j
             y1[j] = dot(w1t_ref[...], xg[s]).astype(BF16)
         for m in range(0, nb, mrows):
             z1[m:m + mrows, :] += (dot(abuf[2 * t, m:m + mrows, :], y1[0], ((1,), (1,)))
@@ -238,40 +241,136 @@
     g2_cp = send(g2.at[0], g2.at[1], 4, 0)
     h1t_cp = send(h1t.at[0], h1t.at[1], 4, 0)
 
-    order = (3, 1, 2, 0)
-    sib2, rcv2 = {}, {}
-
+    half = nb // 2
+    units = ((3, 0), (3, 1), (1, 0), (2, 1), (2, 0), (1, 1), (0, 0), (0, 1))
+
+    def tree(name, g, out, sibb, summ, rfwd, rfar, early):
+        sibs, got = {}, {}
+
+        def cols(h):
+            return slice(h * half, (h + 1) * half)
+
+        def own(q, h, dc):
+            return dot(g[0], abuf[SLOTS[q, dc], :, cols(h)])
+
+        def partner(q, h, dc):
+            return dot(g[1], abuf[SLOTS[q + 4, dc], :, cols(h)])
+
+        def first_dim(h):
+            return 1 if h == 0 else 2
+
+        def begin():
+            for i in range(early):
+                out[i] = own(*units[i], 1)
+                summ[i] = own(*units[i], 0)
+
+        def finish(i):
+            q, h = units[i]
+            with scope(name + "_sib"):
+                sibs[i].wait_recv()
+            summ[i] += sibb[i]
+            if q == 3:
+                got["f", h] = send(summ.at[i], rfwd.at[h], first_dim(h), 0)
+            elif q == first_dim(h):
+                got["x", h] = send(summ.at[i], rfar.at[h], first_dim(h), 0)
+
+        def group(j):
+            pair = (2 * j, 2 * j + 1)
+            with scope(name + "_group"):
+                for i in pair:
+                    if i < early:
+                        out[i] += partner(*units[i], 1)
+                    else:
+                        out[i] = own(*units[i], 1) + partner(*units[i], 1)
+                    sibs[i] = send(out.at[i], sibb.at[i], 0, 1)
+                for i in pair:
+                    if i < early:
+                        summ[i] += partner(*units[i], 0)
+                    else:
+                        summ[i] = own(*units[i], 0) + partner(*units[i], 0)
+            return lambda: [finish(i) for i in pair]
+
+        def forward():
+            for h, i in ((0, 4), (1, 5)):
+                with scope(name + "_fwait"):
+                    got["f", h].wait_recv()
+                summ[i] += rfwd[h]
+                got["y", h] = send(summ.at[i], rfar.at[2 + h], 3 - first_dim(h), 0)
+            for h in (0, 1):
+                with scope(name + "_xwait"):
+                    got["x", h].wait_recv()
+                summ[6 + h] += rfar[h]
+
+        def last(h):
+            with scope(name + "_ywait"):
+                got["y", h].wait_recv()
+            return (summ[6 + h] + rfar[2 + h]).astype(BF16)
+
+        return begin, group, forward, last
+
+    begin, group, forward, last = tree("p2", g2, p2out, p2sib, p2sum, p2fwd, p2far, 8)
     with scope("p2own"):
-        for q in order:
-            p2out[q] = dot(g2[0], abuf[SLOTS[q, 1]])
-            p2sum[q] = dot(g2[0], abuf[SLOTS[q, 0]])
+        begin()
     with scope("g2z_wait"):
         g2_cp.wait_recv()
         for (k, dc), slot in SLOTS.items():
             if k >= 4:
                 a_rows(1 - r, k - 4, dc, slot).wait()
-
-    def fin2(q):
-        with scope("p2sib"):
-            sib2[q].wait_recv()
-        p2sum[q] += p2sib[q]
-        if q:
-            rcv2[q] = send(p2sum.at[q], p2rcv.at[q - 1], q, 0)
-
-    for i, q in enumerate(order):
-        with scope("p2a"):
-            p2out[q] += dot(g2[1], abuf[SLOTS[q + 4, 1]])
-        sib2[q] = send(p2out.at[q], p2sib.at[q], 0, 1)
-        with scope("p2b"):
-            p2sum[q] += dot(g2[1], abuf[SLOTS[q + 4, 0]])
-        if i:
-            fin2(order[i - 1])
-    fin2(0)
-    with scope("p2rcv"):
-        for q in (1, 2, 3):
-            rcv2[q].wait_recv()
-    d2[0] = (p2sum[0] + p2rcv[0] + p2rcv[1] + p2rcv[2]).astype(BF16)
+    for j in range(4):
+        group(j)()
+    forward()
+    for h in (0, 1):
+        d2[0, :, h * half:(h + 1) * half] = last(h)
     d2_cp = send(d2.at[0], d2.at[1], 4, 0)
+
+    def g1_of(i):
+        g1[i] = jnp.where(h1t[i] > 0, dot(w2_ref[...], d2[i]), 0.0).astype(BF16)
+
+    lane = lax.broadcasted_iota(jnp.int32, (hid, cpad), 1)
+    dw2 = dot(h1t[0], d2[0], ((1,), (1,)))
+    part2[:, 0:cpad] = jnp.where(lane == classes, loss_part, dw2)
+    hc, hz = hid // 2, hid // 4
+
+    def span(start, size):
+        return pl.ds(pl.multiple_of(start, size), size)
+
+    cp_c = send(part2.at[span((1 - core) * hc, hc)], rbc, 0, 1)
+    g1_of(0)
+
+    begin, group, forward, last = tree("p6", g1, p6out, p6sib, p6sum, p6fwd, p6far, 2)
+    with scope("p6own"):
+        begin()
+    cp_c.wait_recv()
+    sumc[...] = part2[span(core * hc, hc), :] + rbc[...]
+    cp_z = send(sumc.at[span((1 - r) * hz, hz)], rbz.at[0], 4, 0)
+    with scope("d2z_wait"):
+        h1t_cp.wait_recv()
+        d2_cp.wait_recv()
+    with scope("g1b"):
+        g1_of(1)
+    fin0 = group(0)
+    cp_z.wait_recv()
+    sumz[0] = sumc[span(r * hz, hz), :] + rbz[0]
+    cp_x = send(sumz.at[0], rbz.at[1], 1, 0)
+    fin0()
+    fin1 = group(1)
+    cp_x.wait_recv()
+    sumz[1] = sumz[0] + rbz[1]
+    cp_y = send(sumz.at[1], rbz.at[2], 2, 0)
+    fin1()
+    group(2)()
+    group(3)()
+    forward()
+    mine = span(core * hc + r * hz, hz)
+    cp_y.wait_recv()
+    res2[mine, :] = sumz[1] + rbz[2]
+    cp_z = send(res2.at[mine], res2.at[mine], 4, 0)
+    cp_z.wait_recv()
+    mine = span(core * hc, hc)
+    cp_c = send(res2.at[mine], res2.at[mine], 0, 1)
+    cp_c.wait_recv()
+    o2_ref[...] = res2[...].T[0:classes, :]
+    loss_ref[...] = res2[0:1, classes:classes + 1]
 
     rows = hid // 16
 
@@ -288,86 +387,9 @@
         res[own, :] = acc
         return [send(res.at[own], res.at[own], k, dc) for k, dc in peers]
 
-    def g1_of(i):
-        g1[i] = jnp.where(h1t[i] > 0, dot(w2_ref[...], d2[i]), 0.0).astype(BF16)
-
-    lane = lax.broadcasted_iota(jnp.int32, (hid, cpad), 1)
-    dw2 = dot(h1t[0], d2[0], ((1,), (1,)))
-    part2[:, 0:cpad] = jnp.where(lane == classes, loss_part, dw2)
-    red2 = reduce_start(part2, rb2)
-    g1_of(0)
-
-    half = nb // 2
-    units = ((3, 0), (3, 1), (1, 0), (2, 1), (2, 0), (1, 1), (0, 0), (0, 1))
-    early = 2
-    sib6, got = {}, {}
-
-    def own6(q, h, dc):
-        return dot(g1[0], abuf[SLOTS[q, dc], :, h * half:(h + 1) * half])
-
-    def partner6(q, h, dc):
-        return dot(g1[1], abuf[SLOTS[q + 4, dc], :, h * half:(h + 1) * half])
-
-    def fin6(i):
-        q, h = units[i]
-        with scope("p6sib"):
-            sib6[i].wait_recv()
-        p6sum[i] += p6sib[i]
-        first = 1 if h == 0 else 2
-        if q == 3:
-            got["f", h] = send(p6sum.at[i], r6f.at[h], first, 0)
-        elif q == first:
-            got["x", h] = send(p6sum.at[i], r6x.at[h], first, 0)
-
-    with scope("p6own"):
-        for i in range(early):
-            p6out[i] = own6(*units[i], 1)
-            p6sum[i] = own6(*units[i], 0)
-    with scope("d2z_wait"):
-        h1t_cp.wait_recv()
-        d2_cp.wait_recv()
-    with scope("g1b"):
-        g1_of(1)
-    with scope("p6early"):
-        for i in range(early):
-            p6out[i] += partner6(*units[i], 1)
-            sib6[i] = send(p6out.at[i], p6sib.at[i], 0, 1)
-        for i in range(early):
-            p6sum[i] += partner6(*units[i], 0)
-    for i in range(early):
-        fin6(i)
-    for i in range(early, len(units)):
-        q, h = units[i]
-        with scope("p6a"):
-            p6out[i] = own6(q, h, 1) + partner6(q, h, 1)
-        sib6[i] = send(p6out.at[i], p6sib.at[i], 0, 1)
-        with scope("p6b"):
-            p6sum[i] = own6(q, h, 0) + partner6(q, h, 0)
-        if i > early:
-            fin6(i - 1)
-        if i == early:
-            with scope("red2"):
-                out2 = reduce_mid(part2, rb2, res2, red2)
-    fin6(len(units) - 1)
-    for h, i in ((0, 4), (1, 5)):
-        with scope("f_wait"):
-            got["f", h].wait_recv()
-        p6sum[i] += r6f[h]
-        got["y", h] = send(p6sum.at[i], r6y.at[h], 2 if h == 0 else 1, 0)
-    for h in (0, 1):
-        with scope("x_wait"):
-            got["x", h].wait_recv()
-        p6sum[6 + h] += r6x[h]
-    with scope("out2_wait"):
-        for cp in out2:
-            cp.wait_recv()
-    o2_ref[...] = res2[...].T[0:classes, :]
-    loss_ref[...] = res2[0:1, classes:classes + 1]
     acc = None
     for h in (0, 1):
-        with scope("y_wait"):
-            got["y", h].wait_recv()
-        d1[h] = (p6sum[6 + h] + r6y[h]).astype(BF16)
+        d1[h] = last(h)
         term = dot(d1[h], xg[0, :, h * half:(h + 1) * half], ((1,), (1,)))
         acc = term if acc is None else acc + term
     part1[:, 0:fpad] = acc
@@ -407,11 +429,12 @@
                 V((nb, hid), F32), V((2, hid, nb), BF16), V((16, cpad, nb), BF16), V((nb, lanes), F32), V((2, cpad, nb), BF16),
                 V((f_in, nb), BF16), V((f_in, hid), F32), V((classes, hid), F32), V((1, nb), jnp.int32), V((1, nb), jnp.int32),
                 V((hid, fpad), BF16), V((hid, cpad), BF16), V((cpad, hid), BF16), V((lanes, hid), F32), V((lanes, hid), F32),
-                V((4, cpad, nb), F32), V((4, cpad, nb), F32), V((4, cpad, nb), F32), V((3, cpad, nb), F32),
+                V((8, cpad, half), F32), V((8, cpad, half), F32), V((8, cpad, half), F32), V((2, cpad, half), F32), V((4, cpad, half), F32),
                 V((2, cpad, nb), BF16), V((2, hid, nb), BF16),
                 V((8, hid, half), F32), V((8, hid, half), F32), V((8, hid, half), F32),
-                V((2, hid, half), F32), V((2, hid, half), F32), V((2, hid, half), F32), V((2, hid, half), BF16),
-                V((hid, lanes), F32), V((hid, lanes), F32), V((15, hid // 16, lanes), F32), V((15, hid // 16, lanes), F32),
+                V((2, hid, half), F32), V((4, hid, half), F32), V((2, hid, half), BF16),
+                V((hid, lanes), F32), V((hid, lanes), F32), V((15, hid // 16, lanes), F32), V((hid // 2, lanes), F32),
+                V((3, hid // 4, lanes), F32), V((hid // 2, lanes), F32), V((2, hid // 4, lanes), F32),
                 V((hid, lanes), F32), V((hid, lanes), F32),
                 pltpu.SemaphoreType.DMA((16,)), pltpu.SemaphoreType.DMA((5,)),
                 pltpu.SemaphoreType.DMA((nsem,)), pltpu.SemaphoreType.DMA((nsem,)),

time: 123 us -> 112 us (0.911)
  Pallas kernels: 117 us -> 106 us
    pallas_call x1, Pallas kernels: 117 us -> 106 us  [local_step(): pl.pallas_call(functools.partial(step_kernel, nb, classes, f_in, cpad), o...]
where the time goes in v4:
time: 112 us
  Pallas kernels  106 us (95%)
  local copies, waits for them, and re-layouts  2.97 us (3%)
  between operations  2.4 us (2%)
    pallas_call x1, Pallas kernels, local_step(): pl.pallas_call(functools.partial(step_kernel, nb, classes, f_in, cpad), o...  106 us
    unnamed x2, local copies, waits for them, and re-layouts  2.97 us

profile of v4, /device:TPU:0, one launch (start us, length us, event | category | flops | bytes accessed | tf_op | source)
XLA Modules:
  0.0 111.5 jit_solution(13171842715168061532)
XLA Ops:
  0.6 106.2 %gcn_step.1 = (f32[1,1]{1,0:T(1,128)}, f32[100,256]{1,0:T(8,128)}, f32[47,256]{1,0:T(8,128)}) custom-call(bf16[2048,16384]{1,0:T(8,128)(2,1)} %a_hbm.1, bf16[100,1024]{1,0:T(8,128)(2,1)} %bitcast.6, f32[100,256]{1,0:T(8,128)} %w1_hbm.1, f32[47,256]{1,0:T(8,128)} %bitcast.7, s32[1,1024]{1,0:T(1,128)} %bitcast.9, s32[1,1024]{1,0:T(1,128)} %bitcast.10), custom_call_target="tpu_custom_call" | custom-call | tf_op jit(solution)/shard_map/gcn_step/pallas_call | solution.py:421
  107.4 1.5 %copy.13 = f32[100,256]{1,0:T(8,128)} copy(f32[100,256]{1,0:T(8,128)} %get-tuple-element.13) | data formatting | bytes 204800
  109.0 1.4 %copy.14 = f32[256,47]{0,1:T(8,128)} copy(f32[256,47]{0,1:T(8,128)} %bitcast.8) | data formatting | bytes 96256

commit v5 on v4

v5 whole, which is shorter than its diff:
```python
import functools

import jax
import jax.numpy as jnp
from jax import lax
from jax.experimental import pallas as pl
from jax.experimental.pallas import tpu as pltpu
from jax.sharding import PartitionSpec as P

BF16 = jnp.bfloat16
F32 = jnp.float32
scope = jax.named_scope

ORDERS = ((1, 2, 4), (2, 4, 1), (4, 1, 2))
STAGES = (((0,) * 3,) + tuple(tuple(o[j] for o in ORDERS) for j in range(3))
          + tuple(tuple(o[a] + o[b] for o in ORDERS) for a, b in ((0, 1), (0, 2), (1, 2))) + ((7,) * 3,))
BACK = {key: slot for slot, key in enumerate(
    [(0, 0, 0), (0, 0, 1)] + [(0, k, dc) for k in (3, 1, 2) for dc in (1, 0)] + [(1, k, dc) for k in (3, 1, 2, 0) for dc in (1, 0)])}
COUNT_BASE = 32.0


def dot(a, b, dims=((1,), (0,))):
    return lax.dot_general(a, b, (dims, ((), ())), preferred_element_type=F32)


def step_kernel(nb, classes, f_in, cpad,
                a_hbm, x_hbm, w1_hbm, w2_hbm, lab_hbm, msk_hbm,
                loss_hbm, o1_hbm, o2_hbm,
                abuf, xg, y1, z1, h1t, y2g, z2, g2,
                xraw, w1raw, w2raw, lab_ref, msk_ref, w1t_ref, w2_ref, w2t_ref, w1f, w2f,
                p2out, p2sib, p2sum, p2fwd, p2far, d2, g1,
                p6out, p6sib, p6sum, p6fwd, p6far,
                part1, part2, rb1, rbc, rbz, sumc, sumz, res1, res2, loss_ref, o1_ref, o2_ref,
                asem, psem, osem, ssem, rsem):
    r = lax.axis_index("rep")
    n = lax.axis_index("nodes")
    core = n % 2
    xc = (n // 2) % 2
    yc = n // 4
    hid = z1.shape[1]
    fpad = xg.shape[1]

    def flip(v, f):
        return 1 - v if f else v

    def coords(k, dc):
        rr = flip(r, k // 4)
        nn = flip(yc, (k // 2) % 2) * 4 + flip(xc, k % 2) * 2 + flip(core, dc)
        return rr, nn

    def block_id(k, dc):
        rr, nn = coords(k, dc)
        return nn * 2 + rr

    used = {"send": 0, "recv": 0}
    drains = []

    def new(kind):
        used[kind] += 1
        return used[kind] - 1

    def prepare(src, dst, k, dc, ss, rs):
        return pltpu.make_async_remote_copy(
            src_ref=src, dst_ref=dst, send_sem=ssem.at[ss], recv_sem=rsem.at[rs],
            device_id=coords(k, dc), device_id_type=pl.DeviceIdType.MESH)

    def send(*args):
        prepare(*args).start()

    def landed(ref, rs):
        pltpu.make_async_copy(ref, ref, rsem.at[rs]).wait()

    def drain(ref, ss):
        drains.append((ref, ss))

    peers = [(k, dc) for k in (7, 3, 5, 6, 1, 2, 4, 0) for dc in range(2) if (k, dc) != (0, 0)]

    pre = [pltpu.make_async_copy(src, dst, psem.at[i]) for i, (src, dst) in enumerate(
        ((x_hbm, xraw), (msk_hbm, msk_ref), (w1_hbm, w1raw), (w2_hbm, w2raw), (lab_hbm, lab_ref)))]
    for cp in pre:
        cp.start()
    barrier = pltpu.get_barrier_semaphore()
    near_peers = ((0, 1), (1, 0), (2, 0), (4, 0))
    for k, dc in near_peers:
        pl.semaphore_signal(barrier, inc=1, device_id=coords(k, dc), device_id_type=pl.DeviceIdType.MESH)
    z1[...] = jnp.zeros_like(z1)
    z2[...] = jnp.zeros_like(z2)
    part1[...] = jnp.zeros_like(part1)
    part2[...] = jnp.zeros_like(part2)
    w1f[...] = jnp.zeros_like(w1f)
    w2f[...] = jnp.zeros_like(w2f)
    xg[0] = jnp.zeros((fpad, nb), BF16)
    with scope("entry_x"):
        pre[0].wait()
        pre[1].wait()

    third = (nb // 3 // 128 + 1) * 128
    cuts = [slice(0, third), slice(third, 2 * third), slice(2 * third, nb)]

    def a_load(rows, k, dc, slot, cut=slice(0, nb)):
        row = pl.multiple_of(rows * nb, nb)
        col = pl.multiple_of(block_id(k, dc) * nb + cut.start, 128)
        size = cut.stop - cut.start
        pltpu.make_async_copy(a_hbm.at[pl.ds(row, nb), pl.ds(col, size)], abuf.at[slot, :, cut], asem.at[(slot + 1) // 2]).start()

    def a_wait(base, count, sem):
        pltpu.make_async_copy(a_hbm.at[pl.ds(0, count * nb), pl.ds(0, nb)], a_hbm.at[pl.ds(0, count * nb), pl.ds(0, nb)], asem.at[sem]).wait()

    for slot in range(16):
        t, dc = slot // 2, slot % 2
        if t in (0, 7):
            a_load(r, STAGES[t][0], dc, slot)
        else:
            for p in range(3):
                a_load(r, STAGES[t][p], dc, slot, cuts[p])

    xg[0, 0:f_in, :] = xraw[...]
    count = jnp.sum(msk_ref[...].astype(F32), axis=1, keepdims=True)
    hi = jnp.floor(count * (1.0 / COUNT_BASE))
    lo = count - COUNT_BASE * hi
    row16 = lax.broadcasted_iota(jnp.int32, (16, 128), 0) + (fpad - 16)
    tail = xg[0, fpad - 16:fpad, 0:128].astype(F32)
    tail = jnp.where(row16 == f_in, hi, jnp.where(row16 == f_in + 1, lo, tail))
    xg[0, fpad - 16:fpad, 0:128] = tail.astype(BF16)
    with scope("entry_w"):
        for cp in pre[2:]:
            cp.wait()
    w1f[0:f_in, :] = w1raw[...]
    w1t_ref[...] = w1f[...].T[:, 0:fpad].astype(BF16)
    w2f[0:classes, :] = w2raw[...]
    w2t_ref[...] = w2f[0:cpad, :].astype(BF16)
    w2_ref[...] = w2f[...].T[:, 0:cpad].astype(BF16)
    with scope("entry_barrier"):
        pl.semaphore_wait(barrier, len(near_peers))

    def gather(buf, work, event):
        ss = new("send")
        on = [new("recv") for _ in STAGES]
        ons = [new("recv") for _ in STAGES]

        def piece(slot, p):
            return buf.at[slot, :, cuts[p]]

        for j in range(3):
            for p, order in enumerate(ORDERS):
                send(piece(0, p), piece(2 * (1 + j), p), order[j], 0, ss, on[1 + j])
        sib = [prepare(buf.at[2 * t], buf.at[2 * t + 1], 0, 1, ss, ons[t]) for t in range(8)]
        sib[0].start()
        hops = {1: ((4, 1), (5, 2)), 2: ((6, 2),), 4: ((7, 2),)}
        onward = {t: [prepare(piece(2 * t, p), piece(2 * to, p), order[d], 0, ss, on[to]) for to, d in nxt for p, order in enumerate(ORDERS)]
                  for t, nxt in hops.items()}
        drain(buf.at[pl.ds(0, 15)], ss)
        work(0, 1)

        @pl.loop(1, 8)
        def _(t):
            for u in range(1, 8):
                @pl.when(t == u)
                def _():
                    with scope(f"ev{u}"):
                        landed(buf.at[0], on[u])
                        for cp in onward.get(u, ()):
                            cp.start()
                        sib[u].start()
                        event(u)
                        landed(buf.at[0], ons[u - 1])
            with scope("pair"):
                work(2 * t - 1, 2)
        event(8)
        with scope("ev8"):
            landed(buf.at[0], ons[7])
        work(15, 1)
        event(9)

    mrows = nb // 2

    def z1_work(base, count):
        a_wait(base, count, (base + 1) // 2)
        for j in range(count):
            y1[j] = dot(w1t_ref[...], xg[base + j]).astype(BF16)
        for m in range(0, nb, mrows):
            z1[m:m + mrows, :] += sum(dot(abuf[base + j, m:m + mrows, :], y1[j], ((1,), (1,))) for j in range(count))

    gather(xg, z1_work, lambda t: None)

    with scope("h1y2"):
        for m in range(0, nb, 256):
            h1t[0, :, m:m + 256] = jnp.maximum(z1[m:m + 256, :], 0.0).T.astype(BF16)
        y2g[0] = dot(w2t_ref[...], h1t[0]).astype(BF16)

    def z2_work(base, count):
        for m in range(0, nb, mrows):
            z2[m:m + mrows, 0:cpad] += sum(dot(abuf[base + j, m:m + mrows, :], y2g[base + j], ((1,), (1,))) for j in range(count))

    chunk = hid // 4
    h1t_ss, h1t_rs = new("send"), new("recv")
    h1t_cps = [prepare(h1t.at[0, pl.ds(i * chunk, chunk)], h1t.at[1, pl.ds(i * chunk, chunk)], 4, 0, h1t_ss, h1t_rs) for i in range(4)]
    drain(h1t.at[0], h1t_ss)

    def z2_event(t):
        for (which, k, dc), slot in BACK.items():
            if slot > 1 and (slot + 1) // 2 == t - 1:
                a_load(flip(r, which), k, dc, slot)
        if t == 5:
            h1t_cps[0].start()

    gather(y2g, z2_work, z2_event)

    tails = xg[0, fpad - 16:fpad, 0:128].astype(F32)
    for s in range(1, 16):
        tails = tails + xg[s, fpad - 16:fpad, 0:128].astype(F32)
    at_hi = f_in - (fpad - 16)
    total_m = COUNT_BASE * tails[at_hi:at_hi + 1, 0:1] + tails[at_hi + 1:at_hi + 2, 0:1]
    z2t = z2[...].T[0:cpad, :]
    cls = lax.broadcasted_iota(jnp.int32, (cpad, nb), 0)
    zm = jnp.where(cls < classes, z2t, -jnp.inf)
    zs = zm - jnp.max(zm, axis=0, keepdims=True)
    logp = zs - jnp.log(jnp.sum(jnp.exp(zs), axis=0, keepdims=True))
    hot = cls == lab_ref[...]
    mask_f = msk_ref[...].astype(F32)
    loss_v = -mask_f * jnp.sum(jnp.where(hot, logp, 0.0), axis=0, keepdims=True)
    loss_part = jnp.sum(loss_v, axis=1, keepdims=True) / total_m
    g2[0] = ((jnp.exp(logp) - hot.astype(F32)) * (mask_f / total_m)).astype(BF16)
    g2_rs, g2_ss = new("recv"), new("send")
    send(g2.at[0], g2.at[1], 4, 0, g2_ss, g2_rs)
    drain(g2.at[0], g2_ss)
    for cp in h1t_cps[1:]:
        cp.start()

    half = nb // 2
    units = ((3, 0), (3, 1), (1, 0), (2, 1), (2, 0), (1, 1), (0, 0), (0, 1))

    def tree(name, g, out, sibb, summ, rfwd, rfar, early):
        sib_ss, ss = new("send"), new("send")
        sib_rs = [new("recv") for _ in range(5)]
        f_rs = [new("recv") for _ in range(2)]
        x_rs = new("recv")
        y_rs = [new("recv") for _ in range(2)]
        drain(out, sib_ss)
        drain(summ.at[pl.ds(0, 6)], ss)

        def cols(h):
            return slice(h * half, (h + 1) * half)

        def own(q, h, dc):
            return dot(g[0], abuf[BACK[0, q, dc], :, cols(h)])

        def partner(q, h, dc):
            return dot(g[1], abuf[BACK[1, q, dc], :, cols(h)])

        def first_dim(h):
            return 1 if h == 0 else 2

        def begin():
            for i in range(early):
                out[i] = own(*units[i], 1)
                summ[i] = own(*units[i], 0)

        def finish(i):
            q, h = units[i]
            with scope(name + "_sib"):
                if i < 2:
                    landed(sibb.at[i], sib_rs[i])
                elif i % 2 == 0:
                    landed(sibb.at[pl.ds(i, 2)], sib_rs[1 + i // 2])
            summ[i] += sibb[i]
            if q == 3:
                send(summ.at[i], rfwd.at[h], first_dim(h), 0, ss, f_rs[h])
            elif q == first_dim(h):
                send(summ.at[i], rfar.at[h], first_dim(h), 0, ss, x_rs)

        def group(j):
            pair = (2 * j, 2 * j + 1)
            with scope(name + "_group"):
                for i in pair:
                    if i < early:
                        out[i] += partner(*units[i], 1)
                    else:
                        out[i] = own(*units[i], 1) + partner(*units[i], 1)
                    send(out.at[i], sibb.at[i], 0, 1, sib_ss, sib_rs[i if i < 2 else 1 + i // 2])
                for i in pair:
                    if i < early:
                        summ[i] += partner(*units[i], 0)
                    else:
                        summ[i] = own(*units[i], 0) + partner(*units[i], 0)
            return lambda: [finish(i) for i in pair]

        def forward():
            for h, i in ((0, 4), (1, 5)):
                with scope(name + "_fwait"):
                    landed(rfwd.at[h], f_rs[h])
                summ[i] += rfwd[h]
                for c in range(2):
                    part = (slice(None), slice(c * half // 2, (c + 1) * half // 2))
                    send(summ.at[(i,) + part], rfar.at[(2 + h,) + part], 3 - first_dim(h), 0, ss, y_rs[c])

        def collect():
            with scope(name + "_xwait"):
                landed(rfar.at[pl.ds(0, 2)], x_rs)
            for h in (0, 1):
                summ[6 + h] += rfar[h]

        def last(h, c):
            if h == 0:
                with scope(name + "_ywait"):
                    landed(rfar.at[0], y_rs[c])
            part = (slice(None), slice(c * half // 2, (c + 1) * half // 2))
            return (summ[(6 + h,) + part] + rfar[(2 + h,) + part]).astype(BF16)

        return begin, group, forward, collect, last

    begin, group, forward, collect, last = tree("p2", g2, p2out, p2sib, p2sum, p2fwd, p2far, 8)
    with scope("p2own"):
        for sem in range(1, 5):
            a_wait(0, 1 if sem == 1 else 2, sem)
        begin()
    with scope("g2z_wait"):
        landed(g2.at[1], g2_rs)
        for sem in range(5, 9):
            a_wait(0, 1 if sem == 8 else 2, sem)
    for j in range(3):
        group(j)()
    forward()
    group(3)()
    collect()
    quarters = [(h, c, slice(h * half + c * half // 2, h * half + (c + 1) * half // 2)) for c in (0, 1) for h in (0, 1)]
    d2_rs, d2_ss = new("recv"), new("send")
    for h, c, at in quarters:
        d2[0, :, at] = last(h, c)
        send(d2.at[0, :, at], d2.at[1, :, at], 4, 0, d2_ss, d2_rs)
    drain(d2.at[0], d2_ss)

    def g1_of(i):
        g1[i] = jnp.where(h1t[i] > 0, dot(w2_ref[...], d2[i]), 0.0).astype(BF16)

    lane = lax.broadcasted_iota(jnp.int32, (hid, cpad), 1)
    dw2 = dot(h1t[0], d2[0], ((1,), (1,)))
    part2[:, 0:cpad] = jnp.where(lane == classes, loss_part, dw2)
    hc, hz = hid // 2, hid // 4

    def span(start, size):
        return pl.ds(pl.multiple_of(start, size), size)

    w_ss = new("send")
    w_rs = [new("recv") for _ in range(6)]
    drain(p6out.at[0, :, 0:2 * res2.shape[1]], w_ss)
    send(part2.at[span((1 - core) * hc, hc)], rbc, 0, 1, w_ss, w_rs[0])
    g1_of(0)

    begin, group, forward, collect, last = tree("p6", g1, p6out, p6sib, p6sum, p6fwd, p6far, 2)
    with scope("p6own"):
        begin()
    landed(rbc, w_rs[0])
    sumc[...] = part2[span(core * hc, hc), :] + rbc[...]
    send(sumc.at[span((1 - r) * hz, hz)], rbz.at[0], 4, 0, w_ss, w_rs[1])
    with scope("d2z_wait"):
        landed(h1t.at[1], h1t_rs)
        landed(d2.at[1], d2_rs)
    with scope("g1b"):
        g1_of(1)
    fin0 = group(0)
    landed(rbz.at[0], w_rs[1])
    sumz[0] = sumc[span(r * hz, hz), :] + rbz[0]
    send(sumz.at[0], rbz.at[1], 1, 0, w_ss, w_rs[2])
    fin0()
    fin1 = group(1)
    landed(rbz.at[1], w_rs[2])
    sumz[1] = sumz[0] + rbz[1]
    send(sumz.at[1], rbz.at[2], 2, 0, w_ss, w_rs[3])
    fin1()
    group(2)()
    forward()
    group(3)()
    collect()
    mine = span(core * hc + r * hz, hz)
    landed(rbz.at[2], w_rs[3])
    res2[mine, :] = sumz[1] + rbz[2]
    send(res2.at[mine], res2.at[mine], 4, 0, w_ss, w_rs[4])
    landed(rbz.at[0], w_rs[4])
    mine = span(core * hc, hc)
    send(res2.at[mine], res2.at[mine], 0, 1, w_ss, w_rs[5])
    landed(rbc, w_rs[5])
    o2_ref[...] = res2[...].T[0:classes, :]
    loss_ref[...] = res2[0:1, classes:classes + 1]
    outs = [pltpu.make_async_copy(src, dst, osem.at[i]) for i, (src, dst) in enumerate(
        ((loss_ref, loss_hbm), (o2_ref, o2_hbm), (o1_ref, o1_hbm)))]
    outs[0].start()
    outs[1].start()

    rows = hid // 16

    acc = None
    for h, c, at in quarters:
        term = dot(last(h, c), xg[0, :, at], ((1,), (1,)))
        acc = term if acc is None else acc + term
    part1[:, 0:fpad] = acc
    red_ss = [new("send") for _ in range(2)]
    red_rs = [new("recv") for _ in range(2)]
    with scope("red1"):
        for i, (k, dc) in enumerate(peers):
            send(part1.at[span(block_id(k, dc) * rows, rows)], rb1.at[i], k, dc, red_ss[0], red_rs[0])
        mine = span(block_id(0, 0) * rows, rows)
        landed(rb1, red_rs[0])
        res1[mine, :] = part1[mine, :] + sum(rb1[i] for i in range(len(peers)))
        for k, dc in peers:
            send(res1.at[mine], res1.at[mine], k, dc, red_ss[1], red_rs[1])
    with scope("out1_wait"):
        landed(rb1, red_rs[1])
    drain(rb1, red_ss[0])
    drain(rb1, red_ss[1])
    o1_ref[...] = res1[...].T[0:f_in, :]
    outs[2].start()
    with scope("send_wait"):
        for ref, ss in drains:
            pltpu.make_async_copy(ref, ref, ssem.at[ss]).wait()
        for cp in outs:
            cp.wait()
    assert used == {"send": ssem.shape[0], "recv": rsem.shape[0]}, used


def solution(mesh):
    def local_step(adj_rows, features, w_one, w_two, labels, label_mask):
        nb, f_in = features.shape
        total = adj_rows.shape[1]
        hid, classes = w_two.shape
        cpad = 48
        lanes = 128
        fpad = 112
        half = nb // 2
        nsend, nrecv = 12, 63
        anyspec = pl.BlockSpec(memory_space=pl.ANY)
        V = pltpu.VMEM
        loss, dw1, dw2 = pl.pallas_call(
            functools.partial(step_kernel, nb, classes, f_in, cpad),
            out_shape=[jax.ShapeDtypeStruct((1, 1), F32), jax.ShapeDtypeStruct((f_in, hid), F32),
                       jax.ShapeDtypeStruct((classes, hid), F32)],
            in_specs=[anyspec] * 6,
            out_specs=[anyspec] * 3,
            scratch_shapes=[
                V((total // nb, nb, nb), BF16), V((16, fpad, nb), BF16), V((2, hid, nb), BF16),
                V((nb, hid), F32), V((2, hid, nb), BF16), V((16, cpad, nb), BF16), V((nb, lanes), F32), V((2, cpad, nb), BF16),
                V((f_in, nb), BF16), V((f_in, hid), F32), V((classes, hid), F32), V((1, nb), jnp.int32), V((1, nb), jnp.int32),
                V((hid, fpad), BF16), V((hid, cpad), BF16), V((cpad, hid), BF16), V((lanes, hid), F32), V((lanes, hid), F32),
                V((8, cpad, half), F32), V((8, cpad, half), F32), V((8, cpad, half), F32), V((2, cpad, half), F32), V((4, cpad, half), F32),
                V((2, cpad, nb), BF16), V((2, hid, nb), BF16),
                V((8, hid, half), F32), V((8, hid, half), F32), V((8, hid, half), F32),
                V((2, hid, half), F32), V((4, hid, half), F32),
                V((hid, lanes), F32), V((hid, lanes), F32), V((15, hid // 16, lanes), F32), V((hid // 2, lanes), F32),
                V((3, hid // 4, lanes), F32), V((hid // 2, lanes), F32), V((2, hid // 4, lanes), F32),
                V((hid, lanes), F32), V((hid, lanes), F32), V((1, 1), F32), V((f_in, hid), F32), V((classes, hid), F32),
                pltpu.SemaphoreType.DMA((9,)), pltpu.SemaphoreType.DMA((5,)), pltpu.SemaphoreType.DMA((3,)),
                pltpu.SemaphoreType.DMA((nsend,)), pltpu.SemaphoreType.DMA((nrecv,)),
            ],
            compiler_params=pltpu.CompilerParams(collective_id=0, has_side_effects=True, vmem_limit_bytes=67043328),
            name="gcn_step",
        )(adj_rows, features.T, w_one, w_two.T, labels.reshape(1, nb), label_mask.reshape(1, nb))
        return loss.reshape(()), dw1, dw2.T

    row_spec = P(("nodes", "rep"))
    return jax.shard_map(local_step, mesh=mesh, in_specs=(P("nodes", None), P(("nodes", "rep"), None), P(), P(), row_spec, row_spec), out_specs=(P(), P(), P()), check_vma=False)
```

time: 112 us -> 107 us (0.955)
  Pallas kernels: 106 us -> 102 us
    pallas_call x1, Pallas kernels: 106 us -> 102 us  [local_step(): pl.pallas_call(functools.partial(step_kernel, nb, classes, f_in, cpad), o...]
where the time goes in v5:
time: 107 us
  Pallas kernels  102 us (95%)
  local copies, waits for them, and re-layouts  2.97 us (3%)
  between operations  2.4 us (2%)
    pallas_call x1, Pallas kernels, local_step(): pl.pallas_call(functools.partial(step_kernel, nb, classes, f_in, cpad), o...  102 us
    unnamed x2, local copies, waits for them, and re-layouts  2.97 us

profile of v5, /device:TPU:0, one launch (start us, length us, event | category | flops | bytes accessed | tf_op | source)
XLA Modules:
  0.0 107.1 jit_solution(11446247069523719047)
XLA Ops:
  0.6 101.8 %gcn_step.1 = (f32[1,1]{1,0:T(1,128)}, f32[100,256]{1,0:T(8,128)}, f32[47,256]{1,0:T(8,128)}) custom-call(bf16[2048,16384]{1,0:T(8,128)(2,1)} %a_hbm.1, bf16[100,1024]{1,0:T(8,128)(2,1)} %bitcast.6, f32[100,256]{1,0:T(8,128)} %w1_hbm.1, f32[47,256]{1,0:T(8,128)} %bitcast.7, s32[1,1024]{1,0:T(1,128)} %bitcast.9, s32[1,1024]{1,0:T(1,128)} %bitcast.10), custom_call_target="tpu_custom_call" | custom-call | tf_op jit(solution)/shard_map/gcn_step/pallas_call | solution.py:433
  103.0 1.5 %copy.13 = f32[100,256]{1,0:T(8,128)} copy(f32[100,256]{1,0:T(8,128)} %get-tuple-element.13) | data formatting | bytes 204800
  104.6 1.4 %copy.14 = f32[256,47]{0,1:T(8,128)} copy(f32[256,47]{0,1:T(8,128)} %bitcast.8) | data formatting | bytes 96256

commit v6 on v5

--- a/solution.py
+++ b/solution.py
@@ -101,7 +101,7 @@
         row = pl.multiple_of(rows * nb, nb)
         col = pl.multiple_of(block_id(k, dc) * nb + cut.start, 128)
         size = cut.stop - cut.start
-        pltpu.make_async_copy(a_hbm.at[pl.ds(row, nb), pl.ds(col, size)], abuf.at[slot, :, cut], asem.at[(slot + 1) // 2]).start()
+        pltpu.make_async_copy(a_hbm.at[pl.ds(row, nb), pl.ds(col, size)], abuf.at[slot, :, cut], asem.at[0 if slot < 2 else (slot + 1) // 2]).start()
 
     def a_wait(base, count, sem):
         pltpu.make_async_copy(a_hbm.at[pl.ds(0, count * nb), pl.ds(0, nb)], a_hbm.at[pl.ds(0, count * nb), pl.ds(0, nb)], asem.at[sem]).wait()
@@ -150,20 +150,29 @@
         onward = {t: [prepare(piece(2 * t, p), piece(2 * to, p), order[d], 0, ss, on[to]) for to, d in nxt for p, order in enumerate(ORDERS)]
                   for t, nxt in hops.items()}
         drain(buf.at[pl.ds(0, 15)], ss)
-        work(0, 1)
-
-        @pl.loop(1, 8)
+
+        def arrive(u):
+            with scope(f"ev{u}"):
+                landed(buf.at[0], on[u])
+                for cp in onward.get(u, ()):
+                    cp.start()
+                sib[u].start()
+                event(u)
+                if u > 1:
+                    landed(buf.at[0], ons[u - 1])
+
+        with scope("ev0"):
+            landed(buf.at[0], ons[0])
+        work(0, 2)
+        arrive(1)
+        work(2, 1)
+
+        @pl.loop(2, 8)
         def _(t):
-            for u in range(1, 8):
+            for u in range(2, 8):
                 @pl.when(t == u)
                 def _():
-                    with scope(f"ev{u}"):
-                        landed(buf.at[0], on[u])
-                        for cp in onward.get(u, ()):
-                            cp.start()
-                        sib[u].start()
-                        event(u)
-                        landed(buf.at[0], ons[u - 1])
+                    arrive(u)
             with scope("pair"):
                 work(2 * t - 1, 2)
         event(8)
@@ -175,7 +184,7 @@
     mrows = nb // 2
 
     def z1_work(base, count):
-        a_wait(base, count, (base + 1) // 2)
+        a_wait(base, count, 0 if isinstance(base, int) and base == 0 else (base + 1) // 2)
         for j in range(count):
             y1[j] = dot(w1t_ref[...], xg[base + j]).astype(BF16)
         for m in range(0, nb, mrows):
@@ -232,8 +241,9 @@
 
     def tree(name, g, out, sibb, summ, rfwd, rfar, early):
         sib_ss, ss = new("send"), new("send")
-        sib_rs = [new("recv") for _ in range(5)]
-        f_rs = [new("recv") for _ in range(2)]
+        sib_rs = [new("recv") for _ in range(3)]
+        sibf_rs = {(h, c): new("recv") for h in range(2) for c in range(2)}
+        f_rs = {(h, c): new("recv") for h in range(2) for c in range(2)}
         x_rs = new("recv")
         y_rs = [new("recv") for _ in range(2)]
         drain(out, sib_ss)
@@ -248,6 +258,14 @@
         def partner(q, h, dc):
             return dot(g[1], abuf[BACK[1, q, dc], :, cols(h)])
 
+        def partner_piece(i, dc, c):
+            q, h = units[i]
+            lo = h * half + c * half // 2
+            return dot(g[1], abuf[BACK[1, q, dc], :, lo:lo + half // 2])
+
+        def piece(i, c):
+            return (i, slice(None), slice(c * half // 2, (c + 1) * half // 2))
+
         def first_dim(h):
             return 1 if h == 0 else 2
 
@@ -256,18 +274,23 @@
                 out[i] = own(*units[i], 1)
                 summ[i] = own(*units[i], 0)
 
-        def finish(i):
-            q, h = units[i]
-            with scope(name + "_sib"):
-                if i < 2:
-                    landed(sibb.at[i], sib_rs[i])
-                elif i % 2 == 0:
-                    landed(sibb.at[pl.ds(i, 2)], sib_rs[1 + i // 2])
-            summ[i] += sibb[i]
-            if q == 3:
-                send(summ.at[i], rfwd.at[h], first_dim(h), 0, ss, f_rs[h])
-            elif q == first_dim(h):
-                send(summ.at[i], rfar.at[h], first_dim(h), 0, ss, x_rs)
+        def first_group(between):
+            with scope(name + "_group"):
+                for c in range(2):
+                    for i in range(2):
+                        out[piece(i, c)] += partner_piece(i, 1, c)
+                    for i in range(2):
+                        send(out.at[piece(i, c)], sibb.at[piece(i, c)], 0, 1, sib_ss, sibf_rs[i, c])
+                for i in range(2):
+                    summ[i] += partner(*units[i], 0)
+            for c in range(2):
+                for i in range(2):
+                    with scope(name + "_sib"):
+                        landed(sibb.at[piece(i, c)], sibf_rs[i, c])
+                    summ[piece(i, c)] += sibb[piece(i, c)]
+                    send(summ.at[piece(i, c)], rfwd.at[piece(i, c)], first_dim(i), 0, ss, f_rs[i, c])
+                if c == 0:
+                    between()
 
         def group(j):
             pair = (2 * j, 2 * j + 1)
@@ -277,22 +300,28 @@
                         out[i] += partner(*units[i], 1)
                     else:
                         out[i] = own(*units[i], 1) + partner(*units[i], 1)
-                    send(out.at[i], sibb.at[i], 0, 1, sib_ss, sib_rs[i if i < 2 else 1 + i // 2])
+                for i in pair:
+                    send(out.at[i], sibb.at[i], 0, 1, sib_ss, sib_rs[j - 1])
                 for i in pair:
                     if i < early:
                         summ[i] += partner(*units[i], 0)
                     else:
                         summ[i] = own(*units[i], 0) + partner(*units[i], 0)
-            return lambda: [finish(i) for i in pair]
+            with scope(name + "_sib"):
+                landed(sibb.at[pl.ds(2 * j, 2)], sib_rs[j - 1])
+            for i in pair:
+                q, h = units[i]
+                summ[i] += sibb[i]
+                if q == first_dim(h):
+                    send(summ.at[i], rfar.at[h], first_dim(h), 0, ss, x_rs)
 
         def forward():
-            for h, i in ((0, 4), (1, 5)):
-                with scope(name + "_fwait"):
-                    landed(rfwd.at[h], f_rs[h])
-                summ[i] += rfwd[h]
-                for c in range(2):
-                    part = (slice(None), slice(c * half // 2, (c + 1) * half // 2))
-                    send(summ.at[(i,) + part], rfar.at[(2 + h,) + part], 3 - first_dim(h), 0, ss, y_rs[c])
+            for c in range(2):
+                for h in range(2):
+                    with scope(name + "_fwait"):
+                        landed(rfwd.at[piece(h, c)], f_rs[h, c])
+                    summ[piece(4 + h, c)] += rfwd[piece(h, c)]
+                    send(summ.at[piece(4 + h, c)], rfar.at[piece(2 + h, c)], 3 - first_dim(h), 0, ss, y_rs[c])
 
         def collect():
             with scope(name + "_xwait"):
@@ -304,12 +333,11 @@
             if h == 0:
                 with scope(name + "_ywait"):
                     landed(rfar.at[0], y_rs[c])
-            part = (slice(None), slice(c * half // 2, (c + 1) * half // 2))
-            return (summ[(6 + h,) + part] + rfar[(2 + h,) + part]).astype(BF16)
-
-        return begin, group, forward, collect, last
-
-    begin, group, forward, collect, last = tree("p2", g2, p2out, p2sib, p2sum, p2fwd, p2far, 8)
+            return (summ[piece(6 + h, c)] + rfar[piece(2 + h, c)]).astype(BF16)
+
+        return begin, first_group, group, forward, collect, last
+
+    begin, first_group, group, forward, collect, last = tree("p2", g2, p2out, p2sib, p2sum, p2fwd, p2far, 8)
     with scope("p2own"):
         for sem in range(1, 5):
             a_wait(0, 1 if sem == 1 else 2, sem)
@@ -318,10 +346,11 @@
         landed(g2.at[1], g2_rs)
         for sem in range(5, 9):
             a_wait(0, 1 if sem == 8 else 2, sem)
-    for j in range(3):
-        group(j)()
+    first_group(lambda: None)
+    group(1)
+    group(2)
     forward()
-    group(3)()
+    group(3)
     collect()
     quarters = [(h, c, slice(h * half + c * half // 2, h * half + (c + 1) * half // 2)) for c in (0, 1) for h in (0, 1)]
     d2_rs, d2_ss = new("recv"), new("send")
@@ -347,7 +376,7 @@
     send(part2.at[span((1 - core) * hc, hc)], rbc, 0, 1, w_ss, w_rs[0])
     g1_of(0)
 
-    begin, group, forward, collect, last = tree("p6", g1, p6out, p6sib, p6sum, p6fwd, p6far, 2)
+    begin, first_group, group, forward, collect, last = tree("p6", g1, p6out, p6sib, p6sum, p6fwd, p6far, 2)
     with scope("p6own"):
         begin()
     landed(rbc, w_rs[0])
@@ -358,19 +387,21 @@
         landed(d2.at[1], d2_rs)
     with scope("g1b"):
         g1_of(1)
-    fin0 = group(0)
-    landed(rbz.at[0], w_rs[1])
-    sumz[0] = sumc[span(r * hz, hz), :] + rbz[0]
-    send(sumz.at[0], rbz.at[1], 1, 0, w_ss, w_rs[2])
-    fin0()
-    fin1 = group(1)
-    landed(rbz.at[1], w_rs[2])
+
+    def exchange_x():
+        landed(rbz.at[0], w_rs[1])
+        sumz[0] = sumc[span(r * hz, hz), :] + rbz[0]
+        send(sumz.at[0], rbz.at[1], 1, 0, w_ss, w_rs[2])
+
+    first_group(exchange_x)
+    group(1)
+    group(2)
+    with scope("exchange_y"):
+        landed(rbz.at[1], w_rs[2])
     sumz[1] = sumz[0] + rbz[1]
     send(sumz.at[1], rbz.at[2], 2, 0, w_ss, w_rs[3])
-    fin1()
-    group(2)()
     forward()
-    group(3)()
+    group(3)
     collect()
     mine = span(core * hc + r * hz, hz)
     landed(rbz.at[2], w_rs[3])
@@ -418,6 +449,11 @@
     assert used == {"send": ssem.shape[0], "recv": rsem.shape[0]}, used
 
 
+def copy_kernel(*refs):
+    for src, dst in zip(refs[:3], refs[3:]):
+        dst[...] = src[...]
+
+
 def solution(mesh):
     def local_step(adj_rows, features, w_one, w_two, labels, label_mask):
         nb, f_in = features.shape
@@ -427,7 +463,7 @@
         lanes = 128
         fpad = 112
         half = nb // 2
-        nsend, nrecv = 12, 63
+        nsend, nrecv = 12, 71
         anyspec = pl.BlockSpec(memory_space=pl.ANY)
         V = pltpu.VMEM
         loss, dw1, dw2 = pl.pallas_call(
@@ -454,6 +490,11 @@
             compiler_params=pltpu.CompilerParams(collective_id=0, has_side_effects=True, vmem_limit_bytes=67043328),
             name="gcn_step",
         )(adj_rows, features.T, w_one, w_two.T, labels.reshape(1, nb), label_mask.reshape(1, nb))
+        loss, dw1, dw2 = pl.pallas_call(
+            copy_kernel,
+            out_shape=[jax.ShapeDtypeStruct(v.shape, F32) for v in (loss, dw1, dw2)],
+            name="outputs",
+        )(loss, dw1, dw2)
         return loss.reshape(()), dw1, dw2.T
 
     row_spec = P(("nodes", "rep"))

time: 107 us -> 104 us (0.972)
  local copies, waits for them, and re-layouts: 2.97 us -> 0 us
  between operations: 2.4 us -> 0.64 us
    unnamed x2 -> x0, local copies, waits for them, and re-layouts: 2.97 us -> none
    pallas_call x0 -> x1, Pallas kernels: none -> 2.19 us  [local_step(): pl.pallas_call(copy_kernel, out_shape=[jax.ShapeDtypeStruct(v.shape, F32)...]
    pallas_call x1, Pallas kernels: 102 us -> 101 us  [local_step(): pl.pallas_call(functools.partial(step_kernel, nb, classes, f_in, cpad), o...]
where the time goes in v6:
time: 104 us; the launch traced here: 103 us
  Pallas kernels  103 us (99%)
    pallas_call x1, Pallas kernels, local_step(): pl.pallas_call(functools.partial(step_kernel, nb, classes, f_in, cpad), o...  101 us
    pallas_call x1, Pallas kernels, local_step(): pl.pallas_call(copy_kernel, out_shape=[jax.ShapeDtypeStruct(v.shape, F32)...  2.19 us

profile of v6, /device:TPU:0, one launch (start us, length us, event | category | flops | bytes accessed | tf_op | source)
XLA Modules:
  0.0 103.3 jit_solution(5128766574776017005)
XLA Ops:
  0.6 100.5 %gcn_step.1 = (f32[1,1]{1,0:T(1,128)}, f32[100,256]{1,0:T(8,128)}, f32[47,256]{1,0:T(8,128)}) custom-call(bf16[2048,16384]{1,0:T(8,128)(2,1)} %a_hbm.1, bf16[100,1024]{1,0:T(8,128)(2,1)} %bitcast.6, f32[100,256]{1,0:T(8,128)} %w1_hbm.1, f32[47,256]{1,0:T(8,128)} %bitcast.7, s32[1,1024]{1,0:T(1,128)} %bitcast.8, s32[1,1024]{1,0:T(1,128)} %bitcast.9), custom_call_target="tpu_custom_call" | custom-call | tf_op jit(solution)/shard_map/gcn_step/pallas_call | solution.py:469
  101.2 2.2 %outputs.1 = (f32[1,1]{1,0:T(1,128)}, f32[100,256]{1,0:T(8,128)}, f32[47,256]{1,0:T(8,128)}) custom-call(f32[1,1]{1,0:T(1,128)} %get-tuple-element.9.refs_0_, f32[100,256]{1,0:T(8,128)} %get-tuple-element.10.refs_1_, f32[47,256]{1,0:T(8,128)} %get-tuple-element.11.refs_2_), custom_call_target="tpu_custom_call" | custom-call | tf_op jit(solution)/shard_map/outputs/pallas_call | solution.py:493

commit v7 on v6

--- a/solution.py
+++ b/solution.py
@@ -25,12 +25,12 @@
 
 def step_kernel(nb, classes, f_in, cpad,
                 a_hbm, x_hbm, w1_hbm, w2_hbm, lab_hbm, msk_hbm,
-                loss_hbm, o1_hbm, o2_hbm,
+                o1_hbm, o2_hbm,
                 abuf, xg, y1, z1, h1t, y2g, z2, g2,
                 xraw, w1raw, w2raw, lab_ref, msk_ref, w1t_ref, w2_ref, w2t_ref, w1f, w2f,
                 p2out, p2sib, p2sum, p2fwd, p2far, d2, g1,
                 p6out, p6sib, p6sum, p6fwd, p6far,
-                part1, part2, rb1, rbc, rbz, sumc, sumz, res1, res2, loss_ref, o1_ref, o2_ref,
+                part1, part2, rb1, rbc, rbz, sumc, sumz, res1, res2,
                 asem, psem, osem, ssem, rsem):
     r = lax.axis_index("rep")
     n = lax.axis_index("nodes")
@@ -86,7 +86,6 @@
     z1[...] = jnp.zeros_like(z1)
     z2[...] = jnp.zeros_like(z2)
     part1[...] = jnp.zeros_like(part1)
-    part2[...] = jnp.zeros_like(part2)
     w1f[...] = jnp.zeros_like(w1f)
     w2f[...] = jnp.zeros_like(w2f)
     xg[0] = jnp.zeros((fpad, nb), BF16)
@@ -118,10 +117,10 @@
     count = jnp.sum(msk_ref[...].astype(F32), axis=1, keepdims=True)
     hi = jnp.floor(count * (1.0 / COUNT_BASE))
     lo = count - COUNT_BASE * hi
-    row16 = lax.broadcasted_iota(jnp.int32, (16, 128), 0) + (fpad - 16)
-    tail = xg[0, fpad - 16:fpad, 0:128].astype(F32)
+    row16 = lax.broadcasted_iota(jnp.int32, (8, 128), 0) + (fpad - 8)
+    tail = xg[0, fpad - 8:fpad, 0:128].astype(F32)
     tail = jnp.where(row16 == f_in, hi, jnp.where(row16 == f_in + 1, lo, tail))
-    xg[0, fpad - 16:fpad, 0:128] = tail.astype(BF16)
+    xg[0, fpad - 8:fpad, 0:128] = tail.astype(BF16)
     with scope("entry_w"):
         for cp in pre[2:]:
             cp.wait()
@@ -215,10 +214,10 @@
 
     gather(y2g, z2_work, z2_event)
 
-    tails = xg[0, fpad - 16:fpad, 0:128].astype(F32)
+    tails = xg[0, fpad - 8:fpad, 0:128].astype(F32)
     for s in range(1, 16):
-        tails = tails + xg[s, fpad - 16:fpad, 0:128].astype(F32)
-    at_hi = f_in - (fpad - 16)
+        tails = tails + xg[s, fpad - 8:fpad, 0:128].astype(F32)
+    at_hi = f_in - (fpad - 8)
     total_m = COUNT_BASE * tails[at_hi:at_hi + 1, 0:1] + tails[at_hi + 1:at_hi + 2, 0:1]
     z2t = z2[...].T[0:cpad, :]
     cls = lax.broadcasted_iota(jnp.int32, (cpad, nb), 0)
@@ -362,25 +361,24 @@
     def g1_of(i):
         g1[i] = jnp.where(h1t[i] > 0, dot(w2_ref[...], d2[i]), 0.0).astype(BF16)
 
-    lane = lax.broadcasted_iota(jnp.int32, (hid, cpad), 1)
-    dw2 = dot(h1t[0], d2[0], ((1,), (1,)))
-    part2[:, 0:cpad] = jnp.where(lane == classes, loss_part, dw2)
-    hc, hz = hid // 2, hid // 4
+    cls_row = lax.broadcasted_iota(jnp.int32, (cpad, hid), 0)
+    part2[...] = jnp.where(cls_row == classes, loss_part, dot(d2[0], h1t[0], ((1,), (1,))))
+    hc, hz = hid // 2, cpad // 2
 
     def span(start, size):
         return pl.ds(pl.multiple_of(start, size), size)
 
     w_ss = new("send")
     w_rs = [new("recv") for _ in range(6)]
-    drain(p6out.at[0, :, 0:2 * res2.shape[1]], w_ss)
-    send(part2.at[span((1 - core) * hc, hc)], rbc, 0, 1, w_ss, w_rs[0])
+    drain(p2out.at[0], w_ss)
+    send(part2.at[:, span((1 - core) * hc, hc)], rbc, 0, 1, w_ss, w_rs[0])
     g1_of(0)
 
     begin, first_group, group, forward, collect, last = tree("p6", g1, p6out, p6sib, p6sum, p6fwd, p6far, 2)
     with scope("p6own"):
         begin()
     landed(rbc, w_rs[0])
-    sumc[...] = part2[span(core * hc, hc), :] + rbc[...]
+    sumc[...] = part2[:, span(core * hc, hc)] + rbc[...]
     send(sumc.at[span((1 - r) * hz, hz)], rbz.at[0], 4, 0, w_ss, w_rs[1])
     with scope("d2z_wait"):
         landed(h1t.at[1], h1t_rs)
@@ -403,28 +401,24 @@
     forward()
     group(3)
     collect()
-    mine = span(core * hc + r * hz, hz)
+    mine = (span(r * hz, hz), span(core * hc, hc))
     landed(rbz.at[2], w_rs[3])
-    res2[mine, :] = sumz[1] + rbz[2]
+    res2[mine] = sumz[1] + rbz[2]
     send(res2.at[mine], res2.at[mine], 4, 0, w_ss, w_rs[4])
     landed(rbz.at[0], w_rs[4])
-    mine = span(core * hc, hc)
+    mine = (slice(None), span(core * hc, hc))
     send(res2.at[mine], res2.at[mine], 0, 1, w_ss, w_rs[5])
     landed(rbc, w_rs[5])
-    o2_ref[...] = res2[...].T[0:classes, :]
-    loss_ref[...] = res2[0:1, classes:classes + 1]
-    outs = [pltpu.make_async_copy(src, dst, osem.at[i]) for i, (src, dst) in enumerate(
-        ((loss_ref, loss_hbm), (o2_ref, o2_hbm), (o1_ref, o1_hbm)))]
+    outs = [pltpu.make_async_copy(src, dst, osem.at[i]) for i, (src, dst) in enumerate(((res2, o2_hbm), (res1, o1_hbm)))]
     outs[0].start()
-    outs[1].start()
-
-    rows = hid // 16
+
+    rows = part1.shape[0] // 16
 
     acc = None
     for h, c, at in quarters:
-        term = dot(last(h, c), xg[0, :, at], ((1,), (1,)))
+        term = dot(xg[0, :, at], last(h, c), ((1,), (1,)))
         acc = term if acc is None else acc + term
-    part1[:, 0:fpad] = acc
+    part1[0:fpad, :] = acc
     red_ss = [new("send") for _ in range(2)]
     red_rs = [new("recv") for _ in range(2)]
     with scope("red1"):
@@ -439,8 +433,7 @@
         landed(rb1, red_rs[1])
     drain(rb1, red_ss[0])
     drain(rb1, red_ss[1])
-    o1_ref[...] = res1[...].T[0:f_in, :]
-    outs[2].start()
+    outs[1].start()
     with scope("send_wait"):
         for ref, ss in drains:
             pltpu.make_async_copy(ref, ref, ssem.at[ss]).wait()
@@ -449,9 +442,11 @@
     assert used == {"send": ssem.shape[0], "recv": rsem.shape[0]}, used
 
 
-def copy_kernel(*refs):
-    for src, dst in zip(refs[:3], refs[3:]):
-        dst[...] = src[...]
+def output_kernel(in1_ref, in2_ref, loss_ref, o1_ref, o2_ref):
+    f_in, classes = o1_ref.shape[0], o2_ref.shape[0]
+    o1_ref[...] = in1_ref[0:f_in, :]
+    o2_ref[...] = in2_ref[0:classes, :]
+    loss_ref[...] = in2_ref[classes:classes + 1, 0:1]
 
 
 def solution(mesh):
@@ -461,17 +456,16 @@
         hid, classes = w_two.shape
         cpad = 48
         lanes = 128
-        fpad = 112
+        fpad = 104
         half = nb // 2
         nsend, nrecv = 12, 71
         anyspec = pl.BlockSpec(memory_space=pl.ANY)
         V = pltpu.VMEM
-        loss, dw1, dw2 = pl.pallas_call(
+        dw1, dw2 = pl.pallas_call(
             functools.partial(step_kernel, nb, classes, f_in, cpad),
-            out_shape=[jax.ShapeDtypeStruct((1, 1), F32), jax.ShapeDtypeStruct((f_in, hid), F32),
-                       jax.ShapeDtypeStruct((classes, hid), F32)],
+            out_shape=[jax.ShapeDtypeStruct((lanes, hid), F32), jax.ShapeDtypeStruct((cpad, hid), F32)],
             in_specs=[anyspec] * 6,
-            out_specs=[anyspec] * 3,
+            out_specs=[anyspec] * 2,
             scratch_shapes=[
                 V((total // nb, nb, nb), BF16), V((16, fpad, nb), BF16), V((2, hid, nb), BF16),
                 V((nb, hid), F32), V((2, hid, nb), BF16), V((16, cpad, nb), BF16), V((nb, lanes), F32), V((2, cpad, nb), BF16),
@@ -481,20 +475,21 @@
                 V((2, cpad, nb), BF16), V((2, hid, nb), BF16),
                 V((8, hid, half), F32), V((8, hid, half), F32), V((8, hid, half), F32),
                 V((2, hid, half), F32), V((4, hid, half), F32),
-                V((hid, lanes), F32), V((hid, lanes), F32), V((15, hid // 16, lanes), F32), V((hid // 2, lanes), F32),
-                V((3, hid // 4, lanes), F32), V((hid // 2, lanes), F32), V((2, hid // 4, lanes), F32),
-                V((hid, lanes), F32), V((hid, lanes), F32), V((1, 1), F32), V((f_in, hid), F32), V((classes, hid), F32),
-                pltpu.SemaphoreType.DMA((9,)), pltpu.SemaphoreType.DMA((5,)), pltpu.SemaphoreType.DMA((3,)),
+                V((lanes, hid), F32), V((cpad, hid), F32), V((15, lanes // 16, hid), F32), V((cpad, hid // 2), F32),
+                V((3, cpad // 2, hid // 2), F32), V((cpad, hid // 2), F32), V((2, cpad // 2, hid // 2), F32),
+                V((lanes, hid), F32), V((cpad, hid), F32),
+                pltpu.SemaphoreType.DMA((9,)), pltpu.SemaphoreType.DMA((5,)), pltpu.SemaphoreType.DMA((2,)),
                 pltpu.SemaphoreType.DMA((nsend,)), pltpu.SemaphoreType.DMA((nrecv,)),
             ],
             compiler_params=pltpu.CompilerParams(collective_id=0, has_side_effects=True, vmem_limit_bytes=67043328),
             name="gcn_step",
         )(adj_rows, features.T, w_one, w_two.T, labels.reshape(1, nb), label_mask.reshape(1, nb))
         loss, dw1, dw2 = pl.pallas_call(
-            copy_kernel,
-            out_shape=[jax.ShapeDtypeStruct(v.shape, F32) for v in (loss, dw1, dw2)],
+            output_kernel,
+            out_shape=[jax.ShapeDtypeStruct((1, 1), F32), jax.ShapeDtypeStruct((f_in, hid), F32),
+                       jax.ShapeDtypeStruct((classes, hid), F32)],
             name="outputs",
-        )(loss, dw1, dw2)
+        )(dw1, dw2)
         return loss.reshape(()), dw1, dw2.T
 
     row_spec = P(("nodes", "rep"))

time: 104 us -> 102 us (0.981)
  Pallas kernels: 103 us -> 101 us
    pallas_call x1, Pallas kernels: 101 us -> 99.3 us  [local_step(): pl.pallas_call(functools.partial(step_kernel, nb, classes, f_in, cpad), o...]
where the time goes in v7:
time: 102 us
  Pallas kernels  101 us (99%)
    pallas_call x1, Pallas kernels, local_step(): pl.pallas_call(functools.partial(step_kernel, nb, classes, f_in, cpad), o...  99.3 us

profile of v7, /device:TPU:0, one launch (start us, length us, event | category | flops | bytes accessed | tf_op | source)
XLA Modules:
  0.0 101.6 jit_solution(3864677972523971070)
XLA Ops:
  0.6 99.3 %gcn_step.1 = (f32[128,256]{1,0:T(8,128)}, f32[48,256]{1,0:T(8,128)}) custom-call(bf16[2048,16384]{1,0:T(8,128)(2,1)} %a_hbm.1, bf16[100,1024]{1,0:T(8,128)(2,1)} %bitcast.6, f32[100,256]{1,0:T(8,128)} %w1_hbm.1, f32[47,256]{1,0:T(8,128)} %bitcast.7, s32[1,1024]{1,0:T(1,128)} %bitcast.8, s32[1,1024]{1,0:T(1,128)} %bitcast.9), custom_call_target="tpu_custom_call" | custom-call | tf_op jit(solution)/shard_map/gcn_step/pallas_call | solution.py:464
  100.0 1.6 %outputs.1 = (f32[1,1]{1,0:T(1,128)}, f32[100,256]{1,0:T(8,128)}, f32[47,256]{1,0:T(8,128)}) custom-call(f32[128,256]{1,0:T(8,128)} %get-tuple-element.8.in1_ref, f32[48,256]{1,0:T(8,128)} %get-tuple-element.9.in2_ref), custom_call_target="tpu_custom_call" | custom-call | tf_op jit(solution)/shard_map/outputs/pallas_call | solution.py:487

commit v8 on v7

--- a/solution.py
+++ b/solution.py
@@ -25,13 +25,13 @@
 
 def step_kernel(nb, classes, f_in, cpad,
                 a_hbm, x_hbm, w1_hbm, w2_hbm, lab_hbm, msk_hbm,
-                o1_hbm, o2_hbm,
+                o1_ref, o2_ref,
                 abuf, xg, y1, z1, h1t, y2g, z2, g2,
                 xraw, w1raw, w2raw, lab_ref, msk_ref, w1t_ref, w2_ref, w2t_ref, w1f, w2f,
-                p2out, p2sib, p2sum, p2fwd, p2far, d2, g1,
+                p2out, p2sib, p2sum, p2fwd, p2far, d2,
                 p6out, p6sib, p6sum, p6fwd, p6far,
                 part1, part2, rb1, rbc, rbz, sumc, sumz, res1, res2,
-                asem, psem, osem, ssem, rsem):
+                asem, psem, ssem, rsem):
     r = lax.axis_index("rep")
     n = lax.axis_index("nodes")
     core = n % 2
@@ -187,7 +187,10 @@
         for j in range(count):
             y1[j] = dot(w1t_ref[...], xg[base + j]).astype(BF16)
         for m in range(0, nb, mrows):
-            z1[m:m + mrows, :] += sum(dot(abuf[base + j, m:m + mrows, :], y1[j], ((1,), (1,))) for j in range(count))
+            total = z1[m:m + mrows, :]
+            for j in range(count):
+                total = total + dot(abuf[base + j, m:m + mrows, :], y1[j], ((1,), (1,)))
+            z1[m:m + mrows, :] = total
 
     gather(xg, z1_work, lambda t: None)
 
@@ -198,7 +201,10 @@
 
     def z2_work(base, count):
         for m in range(0, nb, mrows):
-            z2[m:m + mrows, 0:cpad] += sum(dot(abuf[base + j, m:m + mrows, :], y2g[base + j], ((1,), (1,))) for j in range(count))
+            total = z2[m:m + mrows, 0:cpad]
+            for j in range(count):
+                total = total + dot(abuf[base + j, m:m + mrows, :], y2g[base + j], ((1,), (1,)))
+            z2[m:m + mrows, 0:cpad] = total
 
     chunk = hid // 4
     h1t_ss, h1t_rs = new("send"), new("recv")
@@ -280,9 +286,10 @@
                         out[piece(i, c)] += partner_piece(i, 1, c)
                     for i in range(2):
                         send(out.at[piece(i, c)], sibb.at[piece(i, c)], 0, 1, sib_ss, sibf_rs[i, c])
-                for i in range(2):
-                    summ[i] += partner(*units[i], 0)
             for c in range(2):
+                with scope(name + "_group"):
+                    for i in range(2):
+                        summ[piece(i, c)] += partner_piece(i, 0, c)
                 for i in range(2):
                     with scope(name + "_sib"):
                         landed(sibb.at[piece(i, c)], sibf_rs[i, c])
@@ -358,6 +365,8 @@
         send(d2.at[0, :, at], d2.at[1, :, at], 4, 0, d2_ss, d2_rs)
     drain(d2.at[0], d2_ss)
 
+    g1 = y1
+
     def g1_of(i):
         g1[i] = jnp.where(h1t[i] > 0, dot(w2_ref[...], d2[i]), 0.0).astype(BF16)
 
@@ -409,8 +418,7 @@
     mine = (slice(None), span(core * hc, hc))
     send(res2.at[mine], res2.at[mine], 0, 1, w_ss, w_rs[5])
     landed(rbc, w_rs[5])
-    outs = [pltpu.make_async_copy(src, dst, osem.at[i]) for i, (src, dst) in enumerate(((res2, o2_hbm), (res1, o1_hbm)))]
-    outs[0].start()
+    o2_ref[...] = res2[...]
 
     rows = part1.shape[0] // 16
 
@@ -433,12 +441,10 @@
         landed(rb1, red_rs[1])
     drain(rb1, red_ss[0])
     drain(rb1, red_ss[1])
-    outs[1].start()
+    o1_ref[...] = res1[...]
     with scope("send_wait"):
         for ref, ss in drains:
             pltpu.make_async_copy(ref, ref, ssem.at[ss]).wait()
-        for cp in outs:
-            cp.wait()
     assert used == {"send": ssem.shape[0], "recv": rsem.shape[0]}, used
 
 
@@ -463,25 +469,25 @@
         V = pltpu.VMEM
         dw1, dw2 = pl.pallas_call(
             functools.partial(step_kernel, nb, classes, f_in, cpad),
-            out_shape=[jax.ShapeDtypeStruct((lanes, hid), F32), jax.ShapeDtypeStruct((cpad, hid), F32)],
+            out_shape=[V((lanes, hid), F32), V((cpad, hid), F32)],
             in_specs=[anyspec] * 6,
-            out_specs=[anyspec] * 2,
+            out_specs=[pl.BlockSpec(memory_space=pltpu.VMEM)] * 2,
             scratch_shapes=[
                 V((total // nb, nb, nb), BF16), V((16, fpad, nb), BF16), V((2, hid, nb), BF16),
                 V((nb, hid), F32), V((2, hid, nb), BF16), V((16, cpad, nb), BF16), V((nb, lanes), F32), V((2, cpad, nb), BF16),
                 V((f_in, nb), BF16), V((f_in, hid), F32), V((classes, hid), F32), V((1, nb), jnp.int32), V((1, nb), jnp.int32),
                 V((hid, fpad), BF16), V((hid, cpad), BF16), V((cpad, hid), BF16), V((lanes, hid), F32), V((lanes, hid), F32),
                 V((8, cpad, half), F32), V((8, cpad, half), F32), V((8, cpad, half), F32), V((2, cpad, half), F32), V((4, cpad, half), F32),
-                V((2, cpad, nb), BF16), V((2, hid, nb), BF16),
+                V((2, cpad, nb), BF16),
                 V((8, hid, half), F32), V((8, hid, half), F32), V((8, hid, half), F32),
                 V((2, hid, half), F32), V((4, hid, half), F32),
                 V((lanes, hid), F32), V((cpad, hid), F32), V((15, lanes // 16, hid), F32), V((cpad, hid // 2), F32),
                 V((3, cpad // 2, hid // 2), F32), V((cpad, hid // 2), F32), V((2, cpad // 2, hid // 2), F32),
                 V((lanes, hid), F32), V((cpad, hid), F32),
-                pltpu.SemaphoreType.DMA((9,)), pltpu.SemaphoreType.DMA((5,)), pltpu.SemaphoreType.DMA((2,)),
+                pltpu.SemaphoreType.DMA((9,)), pltpu.SemaphoreType.DMA((5,)),
                 pltpu.SemaphoreType.DMA((nsend,)), pltpu.SemaphoreType.DMA((nrecv,)),
             ],
-            compiler_params=pltpu.CompilerParams(collective_id=0, has_side_effects=True, vmem_limit_bytes=67043328),
+            compiler_params=pltpu.CompilerParams(collective_id=0, has_side_effects=True, vmem_limit_bytes=64 * 1000 * 1000),
             name="gcn_step",
         )(adj_rows, features.T, w_one, w_two.T, labels.reshape(1, nb), label_mask.reshape(1, nb))
         loss, dw1, dw2 = pl.pallas_call(
@@ -489,7 +495,7 @@
             out_shape=[jax.ShapeDtypeStruct((1, 1), F32), jax.ShapeDtypeStruct((f_in, hid), F32),
                        jax.ShapeDtypeStruct((classes, hid), F32)],
             name="outputs",
-        )(dw1, dw2)
+        )(*(pltpu.with_memory_space_constraint(v, pltpu.VMEM) for v in (dw1, dw2)))
         return loss.reshape(()), dw1, dw2.T
 
     row_spec = P(("nodes", "rep"))

time: 102 us -> 99.8 us (0.978)
  Pallas kernels: 101 us -> 99 us
    pallas_call x1, Pallas kernels: 99.3 us -> 98.3 us  [local_step(): pl.pallas_call(functools.partial(step_kernel, nb, classes, f_in, cpad), o...]
where the time goes in v8:
time: 99.8 us; the launch traced here: 99.6 us
  Pallas kernels  99 us (99%)
    pallas_call x1, Pallas kernels, local_step(): pl.pallas_call(functools.partial(step_kernel, nb, classes, f_in, cpad), o...  98.3 us

profile of v8, /device:TPU:0, one launch (start us, length us, event | category | flops | bytes accessed | tf_op | source)
XLA Modules:
  0.0 99.6 jit_solution(13903112152999730295)
XLA Ops:
  0.6 98.3 %gcn_step.1 = (f32[128,256]{1,0:T(8,128)S(1)}, f32[48,256]{1,0:T(8,128)S(1)}) custom-call(bf16[2048,16384]{1,0:T(8,128)(2,1)} %a_hbm.1, bf16[100,1024]{1,0:T(8,128)(2,1)} %bitcast.6, f32[100,256]{1,0:T(8,128)} %w1_hbm.1, f32[47,256]{1,0:T(8,128)} %bitcast.7, s32[1,1024]{1,0:T(1,128)} %bitcast.8, s32[1,1024]{1,0:T(1,128)} %bitcast.9), custom_call_target="tpu_custom_call" | custom-call | tf_op jit(solution)/shard_map/gcn_step/pallas_call | solution.py:470
  99.0 0.7 outputs.1

commit v9 on v8

--- a/solution.py
+++ b/solution.py
@@ -132,7 +132,7 @@
     with scope("entry_barrier"):
         pl.semaphore_wait(barrier, len(near_peers))
 
-    def gather(buf, work, event):
+    def gather(buf, work, event, tail=None):
         ss = new("send")
         on = [new("recv") for _ in STAGES]
         ons = [new("recv") for _ in STAGES]
@@ -156,7 +156,6 @@
                 for cp in onward.get(u, ()):
                     cp.start()
                 sib[u].start()
-                event(u)
                 if u > 1:
                     landed(buf.at[0], ons[u - 1])
 
@@ -165,6 +164,7 @@
         work(0, 2)
         arrive(1)
         work(2, 1)
+
 
         @pl.loop(2, 8)
         def _(t):
@@ -172,12 +172,16 @@
                 @pl.when(t == u)
                 def _():
                     arrive(u)
+                    event(u)
             with scope("pair"):
                 work(2 * t - 1, 2)
         event(8)
         with scope("ev8"):
             landed(buf.at[0], ons[7])
-        work(15, 1)
+        if tail:
+            tail()
+        else:
+            work(15, 1)
         event(9)
 
     mrows = nb // 2
@@ -218,26 +222,35 @@
         if t == 5:
             h1t_cps[0].start()
 
-    gather(y2g, z2_work, z2_event)
-
     tails = xg[0, fpad - 8:fpad, 0:128].astype(F32)
     for s in range(1, 16):
         tails = tails + xg[s, fpad - 8:fpad, 0:128].astype(F32)
     at_hi = f_in - (fpad - 8)
     total_m = COUNT_BASE * tails[at_hi:at_hi + 1, 0:1] + tails[at_hi + 1:at_hi + 2, 0:1]
-    z2t = z2[...].T[0:cpad, :]
-    cls = lax.broadcasted_iota(jnp.int32, (cpad, nb), 0)
-    zm = jnp.where(cls < classes, z2t, -jnp.inf)
-    zs = zm - jnp.max(zm, axis=0, keepdims=True)
-    logp = zs - jnp.log(jnp.sum(jnp.exp(zs), axis=0, keepdims=True))
-    hot = cls == lab_ref[...]
-    mask_f = msk_ref[...].astype(F32)
-    loss_v = -mask_f * jnp.sum(jnp.where(hot, logp, 0.0), axis=0, keepdims=True)
-    loss_part = jnp.sum(loss_v, axis=1, keepdims=True) / total_m
-    g2[0] = ((jnp.exp(logp) - hot.astype(F32)) * (mask_f / total_m)).astype(BF16)
     g2_rs, g2_ss = new("recv"), new("send")
-    send(g2.at[0], g2.at[1], 4, 0, g2_ss, g2_rs)
+    losses = []
+
+    def z2_tail():
+        for m in range(0, nb, mrows):
+            at = slice(m, m + mrows)
+            total = z2[at, 0:cpad]
+            total = total + dot(abuf[15, at, :], y2g[15], ((1,), (1,)))
+            z2[at, 0:cpad] = total
+            z2t = z2[at, :].T[0:cpad, :]
+            cls = lax.broadcasted_iota(jnp.int32, (cpad, mrows), 0)
+            zm = jnp.where(cls < classes, z2t, -jnp.inf)
+            zs = zm - jnp.max(zm, axis=0, keepdims=True)
+            logp = zs - jnp.log(jnp.sum(jnp.exp(zs), axis=0, keepdims=True))
+            hot = cls == lab_ref[:, at]
+            mask_f = msk_ref[:, at].astype(F32)
+            loss_v = -mask_f * jnp.sum(jnp.where(hot, logp, 0.0), axis=0, keepdims=True)
+            losses.append(jnp.sum(loss_v, axis=1, keepdims=True))
+            g2[0, :, at] = ((jnp.exp(logp) - hot.astype(F32)) * (mask_f / total_m)).astype(BF16)
+            send(g2.at[0, :, at], g2.at[1, :, at], 4, 0, g2_ss, g2_rs)
+
+    gather(y2g, z2_work, z2_event, z2_tail)
     drain(g2.at[0], g2_ss)
+    loss_part = (losses[0] + losses[1]) / total_m
     for cp in h1t_cps[1:]:
         cp.start()
 
@@ -350,12 +363,14 @@
         begin()
     with scope("g2z_wait"):
         landed(g2.at[1], g2_rs)
-        for sem in range(5, 9):
-            a_wait(0, 1 if sem == 8 else 2, sem)
+        a_wait(0, 2, 5)
     first_group(lambda: None)
+    for sem in (6, 7):
+        a_wait(0, 2, sem)
     group(1)
     group(2)
     forward()
+    a_wait(0, 1, 8)
     group(3)
     collect()
     quarters = [(h, c, slice(h * half + c * half // 2, h * half + (c + 1) * half // 2)) for c in (0, 1) for h in (0, 1)]
@@ -420,7 +435,15 @@
     landed(rbc, w_rs[5])
     o2_ref[...] = res2[...]
 
-    rows = part1.shape[0] // 16
+    rows = rb1.shape[1]
+    owners = part1.shape[0] // rows
+
+    def owner(k, dc):
+        rr, nn = coords(k, dc)
+        chip = rr * 4 + nn // 2
+        return chip, jnp.logical_and(nn % 2 == 1, chip < owners)
+
+    own_id, owns = owner(0, 0)
 
     acc = None
     for h, c, at in quarters:
@@ -429,22 +452,48 @@
     part1[0:fpad, :] = acc
     red_ss = [new("send") for _ in range(2)]
     red_rs = [new("recv") for _ in range(2)]
+    few, most = rb1.at[pl.ds(0, owners - 1)], rb1.at[pl.ds(0, owners)]
     with scope("red1"):
         for i, (k, dc) in enumerate(peers):
-            send(part1.at[span(block_id(k, dc) * rows, rows)], rb1.at[i], k, dc, red_ss[0], red_rs[0])
-        mine = span(block_id(0, 0) * rows, rows)
-        landed(rb1, red_rs[0])
-        res1[mine, :] = part1[mine, :] + sum(rb1[i] for i in range(len(peers)))
-        for k, dc in peers:
-            send(res1.at[mine], res1.at[mine], k, dc, red_ss[1], red_rs[1])
+            peer_id, peer_owns = owner(k, dc)
+
+            @pl.when(peer_owns)
+            def _():
+                send(part1.at[span(peer_id * rows, rows)], rb1.at[i], k, dc, red_ss[0], red_rs[0])
+
+        @pl.when(owns)
+        def _():
+            mine = span(own_id * rows, rows)
+            landed(rb1, red_rs[0])
+            res1[mine, :] = part1[mine, :] + sum(rb1[i] for i in range(len(peers)))
+            for k, dc in peers:
+                send(res1.at[mine], res1.at[mine], k, dc, red_ss[1], red_rs[1])
+
     with scope("out1_wait"):
-        landed(rb1, red_rs[1])
-    drain(rb1, red_ss[0])
-    drain(rb1, red_ss[1])
+        @pl.when(owns)
+        def _():
+            landed(few, red_rs[1])
+
+        @pl.when(jnp.logical_not(owns))
+        def _():
+            landed(most, red_rs[1])
+
     o1_ref[...] = res1[...]
     with scope("send_wait"):
+        def drained(ref, ss):
+            pltpu.make_async_copy(ref, ref, ssem.at[ss]).wait()
+
         for ref, ss in drains:
-            pltpu.make_async_copy(ref, ref, ssem.at[ss]).wait()
+            drained(ref, ss)
+
+        @pl.when(owns)
+        def _():
+            drained(few, red_ss[0])
+            drained(rb1, red_ss[1])
+
+        @pl.when(jnp.logical_not(owns))
+        def _():
+            drained(most, red_ss[0])
     assert used == {"send": ssem.shape[0], "recv": rsem.shape[0]}, used
 
 
@@ -463,13 +512,14 @@
         cpad = 48
         lanes = 128
         fpad = 104
+        frows = 112
         half = nb // 2
         nsend, nrecv = 12, 71
         anyspec = pl.BlockSpec(memory_space=pl.ANY)
         V = pltpu.VMEM
         dw1, dw2 = pl.pallas_call(
             functools.partial(step_kernel, nb, classes, f_in, cpad),
-            out_shape=[V((lanes, hid), F32), V((cpad, hid), F32)],
+            out_shape=[V((frows, hid), F32), V((cpad, hid), F32)],
             in_specs=[anyspec] * 6,
             out_specs=[pl.BlockSpec(memory_space=pltpu.VMEM)] * 2,
             scratch_shapes=[
@@ -481,9 +531,9 @@
                 V((2, cpad, nb), BF16),
                 V((8, hid, half), F32), V((8, hid, half), F32), V((8, hid, half), F32),
                 V((2, hid, half), F32), V((4, hid, half), F32),
-                V((lanes, hid), F32), V((cpad, hid), F32), V((15, lanes // 16, hid), F32), V((cpad, hid // 2), F32),
+                V((frows, hid), F32), V((cpad, hid), F32), V((15, 16, hid), F32), V((cpad, hid // 2), F32),
                 V((3, cpad // 2, hid // 2), F32), V((cpad, hid // 2), F32), V((2, cpad // 2, hid // 2), F32),
-                V((lanes, hid), F32), V((cpad, hid), F32),
+                V((frows, hid), F32), V((cpad, hid), F32),
                 pltpu.SemaphoreType.DMA((9,)), pltpu.SemaphoreType.DMA((5,)),
                 pltpu.SemaphoreType.DMA((nsend,)), pltpu.SemaphoreType.DMA((nrecv,)),
             ],

time: 99.8 us -> 99.1 us (level)
  no operation moved by 1% of the time
where the time goes in v9:
time: 99.1 us; the launch traced here: 99 us
  Pallas kernels  98.4 us (99%)
    pallas_call x1, Pallas kernels, local_step(): pl.pallas_call(functools.partial(step_kernel, nb, classes, f_in, cpad), o...  97.7 us

profile of v9, /device:TPU:0, one launch (start us, length us, event | category | flops | bytes accessed | tf_op | source)
XLA Modules:
  0.0 99.0 jit_solution(13825286468367318516)
XLA Ops:
  0.6 97.7 %gcn_step.1 = (f32[112,256]{1,0:T(8,128)S(1)}, f32[48,256]{1,0:T(8,128)S(1)}) custom-call(bf16[2048,16384]{1,0:T(8,128)(2,1)} %a_hbm.1, bf16[100,1024]{1,0:T(8,128)(2,1)} %bitcast.6, f32[100,256]{1,0:T(8,128)} %w1_hbm.1, f32[47,256]{1,0:T(8,128)} %bitcast.7, s32[1,1024]{1,0:T(1,128)} %bitcast.8, s32[1,1024]{1,0:T(1,128)} %bitcast.9), custom_call_target="tpu_custom_call" | custom-call | tf_op jit(solution)/shard_map/gcn_step/pallas_call | solution.py:520
  98.3 0.7 outputs.1

commit v10 on v9

--- a/solution.py
+++ b/solution.py
@@ -292,14 +292,20 @@
                 out[i] = own(*units[i], 1)
                 summ[i] = own(*units[i], 0)
 
-        def first_group(between):
-            with scope(name + "_group"):
-                for c in range(2):
+        def first_group(between, whole):
+            def form(c):
+                with scope(name + "_group"):
                     for i in range(2):
                         out[piece(i, c)] += partner_piece(i, 1, c)
                     for i in range(2):
                         send(out.at[piece(i, c)], sibb.at[piece(i, c)], 0, 1, sib_ss, sibf_rs[i, c])
+
+            if whole:
+                form(0)
+                form(1)
             for c in range(2):
+                if not whole:
+                    form(c)
                 with scope(name + "_group"):
                     for i in range(2):
                         summ[piece(i, c)] += partner_piece(i, 0, c)
@@ -364,7 +370,7 @@
     with scope("g2z_wait"):
         landed(g2.at[1], g2_rs)
         a_wait(0, 2, 5)
-    first_group(lambda: None)
+    first_group(lambda: None, whole=True)
     for sem in (6, 7):
         a_wait(0, 2, sem)
     group(1)
@@ -415,7 +421,7 @@
         sumz[0] = sumc[span(r * hz, hz), :] + rbz[0]
         send(sumz.at[0], rbz.at[1], 1, 0, w_ss, w_rs[2])
 
-    first_group(exchange_x)
+    first_group(exchange_x, whole=False)
     group(1)
     group(2)
     with scope("exchange_y"):

time: 99.1 us -> 98.6 us (level)
  no operation moved by 1% of the time
where the time goes in v10:
time: 98.6 us; the launch traced here: 98.5 us
  Pallas kernels  97.9 us (99%)
    pallas_call x1, Pallas kernels, local_step(): pl.pallas_call(functools.partial(step_kernel, nb, classes, f_in, cpad), o...  97.2 us

profile of v10, /device:TPU:0, one launch (start us, length us, event | category | flops | bytes accessed | tf_op | source)
XLA Modules:
  0.0 98.5 jit_solution(13292382618040085466)
XLA Ops:
  0.6 97.2 %gcn_step.1 = (f32[112,256]{1,0:T(8,128)S(1)}, f32[48,256]{1,0:T(8,128)S(1)}) custom-call(bf16[2048,16384]{1,0:T(8,128)(2,1)} %a_hbm.1, bf16[100,1024]{1,0:T(8,128)(2,1)} %bitcast.6, f32[100,256]{1,0:T(8,128)} %w1_hbm.1, f32[47,256]{1,0:T(8,128)} %bitcast.7, s32[1,1024]{1,0:T(1,128)} %bitcast.8, s32[1,1024]{1,0:T(1,128)} %bitcast.9), custom_call_target="tpu_custom_call" | custom-call | tf_op jit(solution)/shard_map/gcn_step/pallas_call | solution.py:526
  97.9 0.7 outputs.1

commit v11 on v10

--- a/solution.py
+++ b/solution.py
@@ -317,7 +317,7 @@
                 if c == 0:
                     between()
 
-        def group(j):
+        def group_out(j):
             pair = (2 * j, 2 * j + 1)
             with scope(name + "_group"):
                 for i in pair:
@@ -327,6 +327,12 @@
                         out[i] = own(*units[i], 1) + partner(*units[i], 1)
                 for i in pair:
                     send(out.at[i], sibb.at[i], 0, 1, sib_ss, sib_rs[j - 1])
+
+        def group(j, formed=False):
+            pair = (2 * j, 2 * j + 1)
+            if not formed:
+                group_out(j)
+            with scope(name + "_group"):
                 for i in pair:
                     if i < early:
                         summ[i] += partner(*units[i], 0)
@@ -360,9 +366,9 @@
                     landed(rfar.at[0], y_rs[c])
             return (summ[piece(6 + h, c)] + rfar[piece(2 + h, c)]).astype(BF16)
 
-        return begin, first_group, group, forward, collect, last
-
-    begin, first_group, group, forward, collect, last = tree("p2", g2, p2out, p2sib, p2sum, p2fwd, p2far, 8)
+        return begin, first_group, group_out, group, forward, collect, last
+
+    begin, first_group, group_out, group, forward, collect, last = tree("p2", g2, p2out, p2sib, p2sum, p2fwd, p2far, 8)
     with scope("p2own"):
         for sem in range(1, 5):
             a_wait(0, 1 if sem == 1 else 2, sem)
@@ -370,10 +376,13 @@
     with scope("g2z_wait"):
         landed(g2.at[1], g2_rs)
         a_wait(0, 2, 5)
-    first_group(lambda: None, whole=True)
-    for sem in (6, 7):
-        a_wait(0, 2, sem)
-    group(1)
+    def next_outs():
+        for sem in (6, 7):
+            a_wait(0, 2, sem)
+        group_out(1)
+
+    first_group(next_outs, whole=True)
+    group(1, formed=True)
     group(2)
     forward()
     a_wait(0, 1, 8)
@@ -404,7 +413,7 @@
     send(part2.at[:, span((1 - core) * hc, hc)], rbc, 0, 1, w_ss, w_rs[0])
     g1_of(0)
 
-    begin, first_group, group, forward, collect, last = tree("p6", g1, p6out, p6sib, p6sum, p6fwd, p6far, 2)
+    begin, first_group, _, group, forward, collect, last = tree("p6", g1, p6out, p6sib, p6sum, p6fwd, p6far, 2)
     with scope("p6own"):
         begin()
     landed(rbc, w_rs[0])

time: 98.6 us -> 99.2 us (level)
  no operation moved by 1% of the time
where the time goes in v11:
time: 99.2 us; the launch traced here: 99 us
  Pallas kernels  98.4 us (99%)
    pallas_call x1, Pallas kernels, local_step(): pl.pallas_call(functools.partial(step_kernel, nb, classes, f_in, cpad), o...  97.7 us

profile of v11, /device:TPU:0, one launch (start us, length us, event | category | flops | bytes accessed | tf_op | source)
XLA Modules:
  0.0 99.0 jit_solution(4228836725710845294)
XLA Ops:
  0.6 97.7 %gcn_step.1 = (f32[112,256]{1,0:T(8,128)S(1)}, f32[48,256]{1,0:T(8,128)S(1)}) custom-call(bf16[2048,16384]{1,0:T(8,128)(2,1)} %a_hbm.1, bf16[100,1024]{1,0:T(8,128)(2,1)} %bitcast.6, f32[100,256]{1,0:T(8,128)} %w1_hbm.1, f32[47,256]{1,0:T(8,128)} %bitcast.7, s32[1,1024]{1,0:T(1,128)} %bitcast.8, s32[1,1024]{1,0:T(1,128)} %bitcast.9), custom_call_target="tpu_custom_call" | custom-call | tf_op jit(solution)/shard_map/gcn_step/pallas_call | solution.py:535
  98.4 0.7 outputs.1
